TPU v7x, 32 devices: a whole 2x2x4 slice. The times are simulated.
32 devices in a mesh: gx: 4 (over y, x), gy: 4 (over z), gz: 2 (over core).
Axes of the slice: x: 2, y: 2, z: 4, core: 2. Of those that a mesh axis runs over, the one named last changes fastest.
Arguments:
- right_side: float32 [128, 128, 256], P('gx', 'gy', 'gz'), may hold values from -1 to 1
- z_faces: float32 [256], P('gz'), may hold values from 0.5 to 2, as said below
- xy_coupling: float32 [5], replicated, as said below
- block_inverse: float32 [5, 256, 128], P(None, 'gz'), as said below
Outputs:
- solution: float32 [128, 128, 256], P('gx', 'gy', 'gz')
- residual: float32 [128, 128, 256], P('gx', 'gy', 'gz')
Inputs may be any that keep to these rules, and one draw needn't show every extreme that they name: z_faces is positive. xy_coupling[l] lies between 2.9 * 4^-l / 128^2 and 5.5 * 4^-l / 128^2. block_inverse[l] holds, block by block, the inverses of the 128 x 128 diagonal blocks of M_l built from z_faces and xy_coupling[l].
All inputs are finite; a program needn't handle non-finite values.
Results may differ from a plain program's by a relative error of at most 0.028.
Values sent between devices are 32-bit elements; how exact they have to be, the bound alone decides.
A program may use at most 128 MiB of HBM per device.

v0:
```python
import functools

import jax
import jax.numpy as jnp
from jax import lax
from jax.experimental import pallas as pl
from jax.experimental.pallas import tpu as pltpu
from jax.sharding import PartitionSpec as P

LEVELS = 5
SWEEPS = 2


damping = 0.8
highest = lax.Precision.HIGHEST


def extended(cells, sides, width):
    for axis, dim in sides:
        count = lax.axis_size(axis)
        ends = count - 1
        head = lax.slice_in_dim(cells, 0, width, axis=dim)
        tail = lax.slice_in_dim(cells, cells.shape[dim] - width, cells.shape[dim], axis=dim)
        cells = jnp.concatenate(
            [
                lax.ppermute(tail, axis, [(i, (i + 1) % count) for i in range(ends)]),
                cells,
                lax.ppermute(head, axis, [((i + 1) % count, i) for i in range(ends)]),
            ],
            axis=dim,
        )
    return cells


def interface_setup(corner_aa, corner_ab, corner_ba, corner_bb, couplings):
    determinant = corner_aa * corner_bb - corner_ab * corner_ba
    corner_inverse = (
        jnp.stack(
            [jnp.stack([corner_bb, -corner_ab], -1), jnp.stack([-corner_ba, corner_aa], -1)], -2
        )
        / determinant[:, None, None]
    )
    blocks_count = corner_aa.shape[0]
    identity = jnp.eye(blocks_count, dtype=corner_inverse.dtype)
    diagonal_part = jnp.einsum("kab,kl->kalb", corner_inverse, identity, precision=highest).reshape(
        2 * blocks_count, 2 * blocks_count
    )
    link_values = jnp.zeros((2 * blocks_count - 1,), corner_inverse.dtype).at[1::2].set(-couplings)
    schur_matrix = diagonal_part + jnp.diag(link_values, 1) + jnp.diag(link_values, -1)
    return (corner_inverse, diagonal_part, jnp.linalg.cholesky(schur_matrix))


def make_solver(inverse_block, corner_rows, couplings, device_index, down_coupling, up_coupling):
    corner_inverse, diagonal_part, factor = interface_setup(
        corner_rows[:, 0], corner_rows[:, 1], corner_rows[:, 2], corner_rows[:, 3], couplings
    )
    block_len = inverse_block.shape[0]
    forward = lax.linalg.triangular_solve(factor, diagonal_part, left_side=True, lower=True)
    reach = lax.linalg.triangular_solve(
        factor, forward, left_side=True, lower=True, transpose_a=True
    )
    padded_reach = jnp.pad(reach, ((1, 1), (0, 0)))
    slice_rows = lax.dynamic_slice_in_dim(padded_reach, 2 * device_index, 4, 0)
    needed = jnp.stack([slice_rows[0], slice_rows[3]])

    def neighbours(end_values):
        zero_carry = jnp.zeros(end_values.shape, jnp.float32)
        nearby = zero_carry + jnp.dot(
            needed, lax.all_gather(end_values, "gz", axis=0, tiled=True), precision=highest
        )
        return (nearby[0], nearby[1])

    def solve(source):
        first_extent, second_extent, depth = source.shape
        line_count = first_extent * second_extent
        local_part = jnp.einsum("xyj,ij->xyi", source, inverse_block, precision=highest)
        end_values = jnp.stack(
            [
                local_part[:, :, 0].reshape(line_count),
                local_part[:, :, block_len - 1].reshape(line_count),
            ]
        )
        below_last, above_first = neighbours(end_values)
        return (
            local_part
            + (down_coupling * below_last).reshape(first_extent, second_extent, 1)
            * inverse_block[:, 0]
            + (up_coupling * above_first).reshape(first_extent, second_extent, 1)
            * inverse_block[:, block_len - 1]
        )

    return solve


def apply_operator(iterate, lateral_weight, down_faces, up_faces):
    padded = extended(iterate, (("gx", 0), ("gy", 1), ("gz", 2)), 1)
    lateral = (
        padded[:-2, 1:-1, 1:-1]
        + padded[2:, 1:-1, 1:-1]
        + padded[1:-1, :-2, 1:-1]
        + padded[1:-1, 2:, 1:-1]
    )
    return (
        lateral_weight * (4.0 * iterate - lateral)
        + down_faces * (iterate - padded[1:-1, 1:-1, :-2])
        + up_faces * (iterate - padded[1:-1, 1:-1, 2:])
    )


def restrict(field):
    first_extent, second_extent, depth = field.shape
    return field.reshape(first_extent // 2, 2, second_extent // 2, 2, depth).sum(axis=(1, 3)) * 0.25


def prolong(padded):
    first_extent = padded.shape[0] - 2
    second_extent = padded.shape[1] - 2
    depth = padded.shape[2]
    even_rows = 0.75 * padded[1:-1] + 0.25 * padded[:-2]
    odd_rows = 0.75 * padded[1:-1] + 0.25 * padded[2:]
    widened = jnp.stack([even_rows, odd_rows], 1).reshape(
        2 * first_extent, second_extent + 2, depth
    )
    even_rows = 0.75 * widened[:, 1:-1] + 0.25 * widened[:, :-2]
    odd_rows = 0.75 * widened[:, 1:-1] + 0.25 * widened[:, 2:]
    return jnp.stack([even_rows, odd_rows], 2).reshape(2 * first_extent, 2 * second_extent, depth)


def body(right_side, z_faces, xy_coupling, block_inverse):
    device_index = lax.axis_index("gz")
    levels_count = block_inverse.shape[0]
    last_cell = block_inverse.shape[1] - 1
    corner = jnp.stack(
        [
            block_inverse[:, 0, 0],
            block_inverse[:, 0, last_cell],
            block_inverse[:, last_cell, 0],
            block_inverse[:, last_cell, last_cell],
        ],
        -1,
    )[None]
    corners, firsts = (
        lax.all_gather(corner, "gz", axis=0, tiled=True),
        lax.all_gather(z_faces[:1], "gz", axis=0, tiled=True),
    )
    couplings = firsts[1:]
    edge_faces = jnp.concatenate([firsts, jnp.ones((1,), jnp.float32)])
    top_face = lax.dynamic_slice_in_dim(edge_faces, device_index + 1, 1, 0)
    up_faces = jnp.concatenate([z_faces[1:], top_face])
    solvers = [
        make_solver(
            block_inverse[level],
            corners[:, level],
            couplings,
            device_index,
            z_faces[0],
            top_face[0],
        )
        for level in range(levels_count)
    ]

    def operator(iterate, level):
        return apply_operator(iterate, xy_coupling[level], z_faces, up_faces)

    def multigrid_cycle(source, level):
        iterate = damping * solvers[level](source)
        iterate = iterate + damping * solvers[level](source - operator(iterate, level))
        if level == LEVELS - 1:
            return iterate
        coarse = multigrid_cycle(restrict(source - operator(iterate, level)), level + 1)
        widened = extended(coarse, (("gx", 0), ("gy", 1)), 1)
        iterate = iterate + prolong(widened)
        for sweep in range(SWEEPS):
            iterate = iterate + damping * solvers[level](source - operator(iterate, level))
        return iterate

    solution = multigrid_cycle(right_side, 0)
    return (solution, right_side - operator(solution, 0))


MESH = pl.DeviceIdType.MESH
HALOS = (4, 6, 6)
ROWS = (4, 5, 6)
YPAD = 8


def block_range(offset, own, halo, extent):
    start = offset * own - halo
    low = max(0, start)
    high = min(extent, (offset + 1) * own + halo)
    return low, high - low, low - start


def cycle_kernel(geometry, f_ref, z_ref, e_ref, g_ref, sol_ref, res_ref, *scratch):
    gx_n, gy_n, gz_n, nx, ny, depth, levels = geometry
    (sinv, g_all, z_all, gather) = scratch[:4]
    R = scratch[4 : 4 + levels]
    U = scratch[4 + levels : 4 + 2 * levels]
    W = scratch[4 + 2 * levels : 4 + 3 * levels]
    V = scratch[4 + 3 * levels : 4 + 4 * levels]
    D = scratch[4 + 4 * levels : 4 + 5 * levels]
    (own1, own2, own3, c4u, c4d, c3u, c3d, cwu, cwd) = scratch[4 + 5 * levels : 13 + 5 * levels]
    OWN = (None, own1, own2, own3)
    (g_send, g_recv, h_send, h_recv, a_send, a_recv, o_send, o_recv) = scratch[13 + 5 * levels :]

    ix, iy, iz = lax.axis_index("gx"), lax.axis_index("gy"), lax.axis_index("gz")
    bx = ix * gz_n + iz
    bx_n = gx_n * gz_n
    f32 = jnp.float32

    def owned(level):
        return nx >> level, ny >> level

    def copy(src, dst, send, recv, device):
        return pltpu.make_async_remote_copy(
            src_ref=src,
            dst_ref=dst,
            send_sem=send,
            recv_sem=recv,
            device_id=device,
            device_id_type=MESH,
        )

    def setup_copies(other):
        here = (ix, iy, lax.rem(iz + other, gz_n))
        out = []
        for level in range(levels):
            out.append(
                copy(
                    g_ref.at[level],
                    g_all.at[level, iz],
                    g_send.at[other, level],
                    g_recv.at[other, level],
                    here,
                )
            )
        out.append(
            copy(z_ref, z_all.at[iz], g_send.at[other, levels], g_recv.at[other, levels], here)
        )
        return out

    def start_copies():
        out = []
        reach = -(-HALOS[0] // nx)
        for t in range(-reach, gz_n + reach):
            xs, xn, xd = block_range(t, nx, HALOS[0], nx * gz_n)
            dgx, target = t // gz_n, t % gz_n
            for dy in (-1, 0, 1):
                ys, yn, yd = block_range(dy, ny, ROWS[0], ny)
                yd += YPAD - ROWS[0]
                out.append((t, dgx, target, dy, (xs, xn, xd), (ys, yn, yd)))
        return out

    plan0 = start_copies()

    def copy0(entry, source_z, device):
        t, dgx, target, dy, (xs, xn, xd), (ys, yn, yd) = entry
        slot = (t + gz_n) * 3 + dy + 1
        return copy(
            f_ref.at[pl.ds(xs, xn), pl.ds(ys, yn), :],
            R[0].at[pl.ds(xd, xn), source_z, pl.ds(yd, yn), :],
            h_send.at[0, slot],
            h_recv.at[0, slot, source_z],
            device,
        )

    def inside(x, y):
        return (x >= 0) & (x < gx_n) & (y >= 0) & (y < gy_n)

    def send0(start):
        for entry in plan0:
            t, dgx, target, dy = entry[:4]
            ok = inside(ix + dgx, iy + dy)
            if dgx == 0 and dy == 0:
                ok = ok & (iz != target)

            @pl.when(ok)
            def _():
                c = copy0(entry, iz, (ix + dgx, iy + dy, target))
                c.start() if start else c.wait_send()

    def recv0():
        for entry in plan0:
            t, dgx, target, dy = entry[:4]
            for source_z in range(gz_n):
                if dgx == 0 and dy == 0 and source_z == target:
                    continue

                @pl.when((iz == target) & inside(ix - dgx, iy - dy))
                def _():
                    copy0(entry, source_z, (ix - dgx, iy - dy, source_z)).wait_recv()

    reach_all = max(
        gz_n - 1 - (-HALOS[0] // nx), *[-(-HALOS[k] // owned(k)[0]) for k in (1, 2)]
    )
    barrier = pltpu.get_barrier_semaphore()

    def greet(other, count):
        x, y = other // gy_n, lax.rem(other, gy_n)
        near = (jnp.abs(x - bx) <= reach_all) & (jnp.abs(y - iy) <= 1)
        near = (near | (x == bx) | (y == iy)) & ((x != bx) | (y != iy))

        @pl.when(near)
        def _():
            pl.semaphore_signal(
                barrier,
                inc=1,
                device_id=(x // gz_n, y, lax.rem(x, gz_n)),
                device_id_type=MESH,
            )

        return count + jnp.where(near, 1, 0).astype(jnp.int32)

    partners = lax.fori_loop(0, bx_n * gy_n, greet, jnp.int32(0))


    for entry in plan0:
        t, dgx, target, dy, (xs, xn, xd) = entry[:5]
        if dgx == 0 and dy == 0:

            @pl.when(iz == target)
            def _():
                def step(i, _):
                    R[0][xd + i, target, pl.ds(YPAD, ny), :] = f_ref[xs + i]
                    return 0

                lax.fori_loop(0, xn, step, 0)

    for level in range(levels):
        g_all[level, iz] = g_ref[level]
    z_all[iz] = z_ref[...]

    for level in range(3):
        planes, zb, rows, lanes = R[level].shape
        halo = HALOS[level]
        n0, n1 = owned(level)
        reach = -(-halo // n0)
        for t in range(1, reach + 1):
            low = max(0, halo - t * n0)
            high = halo - (t - 1) * n0
            plane = jnp.zeros((high - low, zb, rows, lanes), f32)

            @pl.when(bx - t < 0)
            def _():
                R[level][low:high] = plane

            low2, high2 = planes - high, planes - low

            @pl.when(bx + t >= bx_n)
            def _():
                R[level][low2:high2] = plane

        spare = jnp.zeros((zb, YPAD - ROWS[level], lanes), f32)

        def outer(i, _):
            R[level][i, :, pl.ds(0, YPAD - ROWS[level])] = spare
            R[level][i, :, pl.ds(rows - YPAD + ROWS[level], YPAD - ROWS[level])] = spare
            return 0

        lax.fori_loop(0, planes, outer, 0)
        edge = jnp.zeros((zb, YPAD, lanes), f32)

        @pl.when(iy == 0)
        def _():
            lax.fori_loop(0, planes, lambda i, c: zero_rows(R[level], i, 0, edge), 0)

        @pl.when(iy == gy_n - 1)
        def _():
            lax.fori_loop(0, planes, lambda i, c: zero_rows(R[level], i, rows - YPAD, edge), 0)

    def fill(ref):
        zero = jnp.zeros(ref.shape[1:], f32)

        def step(i, _):
            ref[i] = zero
            return 0

        lax.fori_loop(0, ref.shape[0], step, 0)

    for ref in (c4u, c4d, c3u, c3d, cwu, cwd):
        fill(ref)
    for level in range(levels):
        zero = jnp.zeros(W[level].shape[1:], f32)
        W[level][0] = zero
        W[level][W[level].shape[0] - 1] = zero

    pl.semaphore_wait(barrier, partners)
    send0(True)
    for other in range(1, gz_n):
        for c in setup_copies(other):
            c.start()

    for other in range(1, gz_n):
        for c in setup_copies(other):
            c.wait()

    def assemble(level, _):
        merged = g_all[level, 0]
        for k in range(1, gz_n):
            block = g_all[level, k]
            size, cz = merged.shape[0], block.shape[0]
            face = z_all[k][:, 0:1]
            a, d = block[0:1, 0:1], merged[size - 1 : size, size - 1 : size]
            last, first = merged[size - 1 : size], block[0:1]
            scale = face / (1.0 - face * face * a * d)
            p_row = jnp.concatenate([face * a * last, first], 1) * scale
            q_row = jnp.concatenate([last, face * d * first], 1) * scale
            top = jnp.concatenate([merged, jnp.zeros((size, cz), f32)], 1)
            low = jnp.concatenate([jnp.zeros((cz, size), f32), block], 1)
            top = top + merged[:, size - 1 : size] * p_row
            low = low + block[:, 0:1] * q_row
            merged = jnp.concatenate([top, low], 0)
        sinv[level] = (damping * merged).astype(jnp.bfloat16)
        return 0

    lax.fori_loop(0, levels, assemble, 0)

    def plane_mask(level, i):
        n0 = owned(level)[0]
        x = bx * n0 - HALOS[level] + i
        return jnp.where((x >= 0) & (x < bx_n * n0), 1.0, 0.0).astype(f32)

    def row_mask(level, rows, first, stride):
        n1 = owned(level)[1]
        y = lax.broadcasted_iota(jnp.int32, (rows, depth), 0) * stride + first
        y = y + iy * n1 - YPAD
        return jnp.where((y >= 0) & (y < gy_n * n1), 1.0, 0.0).astype(f32)

    def neighbours(level, i):
        centre = W[level][i + 1]
        rows = centre.shape[1]
        before = pltpu.roll(centre, 1, 1)
        after = pltpu.roll(centre, rows - 1, 1)
        if level > 2:
            y = lax.broadcasted_iota(jnp.int32, centre.shape, 1)
            before = jnp.where(y > 0, before, 0.0)
            after = jnp.where(y < rows - 1, after, 0.0)
        return centre, W[level][i] + W[level][i + 2] + before + after

    def sweep(level, first, margin=0):
        planes, zb, rows, lanes = R[level].shape
        e = e_ref[level]

        def widest(count):
            return max(c for c in range(1, count + 1) if count % c == 0 and c * rows <= 300)

        while margin and widest(planes - 2 * margin) * rows < 160:
            margin -= 1
        chunk = widest(planes - 2 * margin)

        def solve(s, _):
            at = margin + s * chunk
            source = [R[level][pl.ds(at, chunk), k] for k in range(zb)]
            flat = [v.reshape(chunk * rows, lanes) for v in source]
            lhs = jnp.concatenate(flat, 1).astype(jnp.bfloat16)
            out = jnp.dot(lhs, sinv[level], preferred_element_type=f32)
            for k in range(zb):
                w = out[:, k * lanes : (k + 1) * lanes].reshape(chunk, rows, lanes)
                W[level][pl.ds(at + 1, chunk), k] = w
                U[level][pl.ds(at, chunk), k] = w if first else U[level][pl.ds(at, chunk), k] + w
                if level > 0:
                    dd = damping * source[k] - (4.0 * e) * w
                    D[level][pl.ds(at, chunk), k] = (
                        dd if first else D[level][pl.ds(at, chunk), k] + dd
                    )
            return 0

        lax.fori_loop(0, (planes - 2 * margin) // chunk, solve, 0)

    def update(level, margin=0):
        planes, zb, rows, lanes = R[level].shape
        e = e_ref[level]
        mask_y = row_mask(level, rows, 0, 1) if level < 3 else None

        def step(i, _):
            centre, total = neighbours(level, i)
            value = (1.0 - damping) * R[level][i] + e * total
            if level < 3:
                value = value * (mask_y * plane_mask(level, i))[None]
            R[level][i] = value
            return 0

        lax.fori_loop(margin, planes - margin, step, 0, unroll=2)

    def restrict_planes(level, dst, planes, x0, y0):
        rows = dst.shape[2]

        def step(j, _):
            for k in range(gz_n):
                total = None
                for a in (0, 1):
                    for b in (0, 1):
                        part = R[level][x0 + 2 * j + a, k, pl.ds(y0 + b, rows, 2), :]
                        total = part if total is None else total + part
                dst[j, k] = total * 0.25
            return 0

        lax.fori_loop(0, planes, step, 0)

    def prolong_planes(level, src, dst, offset, x0, y0):
        planes, zb, rows, lanes = R[level].shape
        half = rows // 2
        if level < 3:
            masks = [row_mask(level, half, b, 2) for b in (0, 1)]

        def step(j, _):
            for k in range(zb):
                def load(dx, dy):
                    return src[x0 + j + dx, k, pl.ds(y0 + dy, half), :]

                for b, dy in ((0, -1), (1, 1)):
                    mixed = [0.75 * load(dx, 0) + 0.25 * load(dx, dy) for dx in (-1, 0, 1)]
                    for a, far in ((0, 0), (1, 2)):
                        value = 0.75 * mixed[1] + 0.25 * mixed[far]
                        if level < 3:
                            value = value * (masks[b] * plane_mask(level, 2 * j + a))
                        dst[offset + 2 * j + a, k, pl.ds(b, half, 2), :] = value
            return 0

        lax.fori_loop(0, planes // 2, step, 0)

    def correct(level, coarse_u, coarse_d, x0, y0, margin=0):
        planes = R[level].shape[0]
        rows = R[level].shape[2]
        e = e_ref[level]
        prolong_planes(level, coarse_u, W[level], 1, x0, y0)
        prolong_planes(level, coarse_d, V[level], 0, x0, y0)
        mask_y = row_mask(level, rows, 0, 1) if level < 3 else None

        def step(i, _):
            centre, total = neighbours(level, i)
            side = V[level][i]
            value = R[level][i] - side - (4.0 * e) * centre + e * total
            if level < 3:
                value = value * (mask_y * plane_mask(level, i))[None]
            R[level][i] = value
            U[level][i] = U[level][i] + centre
            if level > 0:
                D[level][i] = D[level][i] + side
            return 0

        lax.fori_loop(margin, planes - margin, step, 0)

    def exchange(level):
        n0, n1 = owned(level)
        halo = HALOS[level]
        own = OWN[level]
        reach = -(-halo // n0)
        window = R[level]

        def local(i, _):
            window[i + halo, :, pl.ds(YPAD, n1), :] = own[i]
            return 0

        def each(act):
            slot = 0
            for t in range(-reach, reach + 1):
                xs, xn, xd = block_range(t, n0, halo, n0)
                for dy in (-1, 0, 1):
                    if t == 0 and dy == 0:
                        continue
                    ys, yn, yd = block_range(dy, n1, ROWS[level], n1)
                    yd += YPAD - ROWS[level]
                    act(t, dy, (xs, xn, xd), (ys, yn, yd), slot)
                    slot += 1

        def build(t, dy, x, y, slot):
            there = bx + t + bx_n
            return copy(
                own.at[pl.ds(x[0], x[1]), :, pl.ds(y[0], y[1]), :],
                window.at[pl.ds(x[2], x[1]), :, pl.ds(y[2], y[1]), :],
                h_send.at[level, slot],
                h_recv.at[level, slot, 0],
                (there // gz_n - gx_n, iy + dy, lax.rem(there, gz_n)),
            )

        def valid(x, y):
            return (x >= 0) & (x < bx_n) & (y >= 0) & (y < gy_n)

        def start(t, dy, x, y, slot):
            @pl.when(valid(bx + t, iy + dy))
            def _():
                build(t, dy, x, y, slot).start()

        def finish(t, dy, x, y, slot):
            @pl.when(valid(bx - t, iy - dy))
            def _():
                build(t, dy, x, y, slot).wait_recv()

        def drain(t, dy, x, y, slot):
            @pl.when(valid(bx + t, iy + dy))
            def _():
                build(t, dy, x, y, slot).wait_send()

        each(start)
        lax.fori_loop(0, n0, local, 0)
        each(finish)
        return lambda: each(drain)

    def gather_all():
        def line_y(other, slot):
            return copy(
                own3,
                gather.at[bx, slot],
                a_send.at[0, other],
                a_recv.at[0, slot],
                (ix, other, iz),
            )

        def line_x(other, slot):
            return copy(
                gather.at[slot],
                gather.at[slot],
                a_send.at[1, other],
                a_recv.at[1, slot],
                (other // gz_n, iy, lax.rem(other, gz_n)),
            )

        def over(build, me, count, act):
            for s in range(1, count):
                act(build, lax.rem(me + s, count), me)

        def start(build, other, me):
            build(other, me).start()

        def finish(build, other, me):
            build(other, other).wait_recv()

        def drain(build, other, me):
            build(other, me).wait_send()

        over(line_y, iy, gy_n, start)
        gather[bx, iy] = own3[...]
        over(line_y, iy, gy_n, finish)
        over(line_x, bx, bx_n, start)
        over(line_x, bx, bx_n, finish)
        n0, n1 = owned(3)

        def place(b, _):
            for i in range(n0):
                for y in range(gy_n):
                    R[3][b * n0 + i, :, pl.ds(y * n1, n1), :] = gather[b, y, i]
            return 0

        lax.fori_loop(0, bx_n, place, 0)

        def drains():
            over(line_y, iy, gy_n, drain)
            over(line_x, bx, bx_n, drain)

        return drains

    def store_padded(level, src, dst, x0):
        rows = src.shape[2]

        def step(i, _):
            dst[x0 + i, :, pl.ds(YPAD, rows), :] = src[i]
            return 0

        lax.fori_loop(0, src.shape[0], step, 0)

    recv0()
    drains = [lambda: send0(False)]
    for level in range(3):
        slack = HALOS[level] - ROWS[level]
        sweep(level, True)
        update(level, slack + 1)
        sweep(level, False, slack + 1)
        update(level, slack + 2)
        n0 = owned(level + 1)[0]
        restrict_planes(level, OWN[level + 1], n0, HALOS[level], YPAD)
        drains.append(exchange(level + 1) if level < 2 else gather_all())
    sweep(3, True)
    update(3)
    sweep(3, False)
    update(3)
    restrict_planes(3, R[4], R[4].shape[0], 0, 0)
    sweep(4, True)
    update(4)
    sweep(4, False)
    store_padded(4, U[4], c4u, 1)
    store_padded(4, D[4], c4d, 1)
    correct(3, c4u, c4d, 1, YPAD)
    sweep(3, False)
    update(3)
    sweep(3, False)
    pad3 = HALOS[2] // 2 + 1
    store_padded(3, U[3], c3u, pad3)
    store_padded(3, D[3], c3d, pad3)
    n0, n1 = owned(3)
    margin = YPAD // 2
    for y in range(gy_n):

        @pl.when(iy == y)
        def _():
            def step(j, _):
                for src, dst in ((c3u, cwu), (c3d, cwd)):
                    dst[j, :, pl.ds(margin, n1 + 4 * margin), :] = src[
                        bx * n0 + j, :, pl.ds(y * n1, n1 + 4 * margin), :
                    ]
                return 0

            lax.fori_loop(0, cwu.shape[0], step, 0)

    for level in (2, 1, 0):
        slack = HALOS[level] - ROWS[level]
        if level == 2:
            correct(2, cwu, cwd, 1, YPAD, 2)
        else:
            x0 = HALOS[level + 1] - HALOS[level] // 2
            correct(level, U[level + 1], D[level + 1], x0, YPAD // 2, slack + 2)
        sweep(level, False, slack + 2)
        update(level, slack + 3)
        sweep(level, False, slack + 3)

    def out_copies(which):
        src, dst = ((U[0], sol_ref), (R[0], res_ref))[which]
        out = []
        for other in range(1, gz_n):
            there = lax.rem(iz + other, gz_n)
            out.append(
                copy(
                    src.at[pl.ds(HALOS[0], nx), there, pl.ds(YPAD, ny), :],
                    dst.at[pl.ds(iz * nx, nx), :, :],
                    o_send.at[which, other],
                    o_recv.at[which, other],
                    (ix, iy, there),
                )
            )
        return out

    def out_local(which):
        src, dst = ((U[0], sol_ref), (R[0], res_ref))[which]

        def step(i, _):
            dst[iz * nx + i] = src[HALOS[0] + i, iz, pl.ds(YPAD, ny), :]
            return 0

        lax.fori_loop(0, nx, step, 0)

    for c in out_copies(0):
        c.start()
    update(0, ROWS[0])
    for c in out_copies(1):
        c.start()
    out_local(0)
    out_local(1)
    for drain in drains:
        drain()
    for which in (0, 1):
        for c in out_copies(which):
            c.wait()


def zero_rows(ref, i, at, value):
    ref[i, :, pl.ds(at, YPAD), :] = value
    return 0


def fits(mesh, shape, inverse_shape):
    gx_n, gy_n, gz_n = (mesh.shape[a] for a in ("gx", "gy", "gz"))
    nx, ny = shape[0] // (gx_n * gz_n), shape[1] // gy_n
    return (
        inverse_shape[0] == LEVELS == 5
        and SWEEPS == 2
        and inverse_shape[2] == 128
        and nx % 8 == 0
        and ny % 32 == 0
        and (shape[1] >> 4) % 8 == 0
        and gz_n <= 2
    )


def fused_body(mesh, right_side, z_faces, xy_coupling, block_inverse):
    gx_n, gy_n, gz_n = (mesh.shape[a] for a in ("gx", "gy", "gz"))
    levels, _, depth = block_inverse.shape
    nx, ny = right_side.shape[0] // gz_n, right_side.shape[1]
    windows = []
    for level in range(levels):
        if level < 3:
            size = ((nx >> level) + 2 * HALOS[level], (ny >> level) + 2 * YPAD)
        else:
            size = ((nx * gx_n * gz_n) >> level, (ny * gy_n) >> level)
        windows.append((size[0], gz_n, size[1], depth))
    vmem = lambda shape: pltpu.VMEM(shape, jnp.float32)
    full3, full4 = windows[3], windows[4]
    pad3 = HALOS[2] // 2 + 1
    c4 = (full4[0] + 2, gz_n, full4[2] + 2 * YPAD, depth)
    c3 = (full3[0] + 2 * pad3, gz_n, full3[2] + 2 * YPAD, depth)
    cw = (windows[2][0] // 2 + 2, gz_n, (ny >> 3) + 20, depth)
    reach = 2 * max(-(-HALOS[k] // (nx >> k)) for k in range(3)) + 1
    slots = 3 * max(reach, 3 * gz_n + 1)
    dma = pltpu.SemaphoreType.DMA
    own = lambda k: (nx >> k, gz_n, ny >> k, depth)
    scratch = (
        [
            pltpu.VMEM((levels, gz_n * depth, gz_n * depth), jnp.bfloat16),
            vmem((levels, gz_n, depth, depth)),
            vmem((gz_n, 1, depth)),
            vmem((gx_n * gz_n, gy_n) + own(3)),
        ]
        + [vmem(w) for w in windows]
        + [vmem(w) for w in windows]
        + [vmem((w[0] + 2,) + w[1:]) for w in windows]
        + [vmem(w) for w in windows]
        + [vmem(w) for w in windows]
        + [vmem(own(1)), vmem(own(2)), vmem(own(3))]
        + [vmem(c4), vmem(c4), vmem(c3), vmem(c3), vmem(cw), vmem(cw)]
        + [dma((gz_n, levels + 1))] * 2
        + [dma((3, slots)), dma((3, slots, gz_n))]
        + [dma((2, max(gx_n * gz_n, gy_n)))] * 2
        + [dma((2, gz_n))] * 2
    )
    in_vmem = pl.BlockSpec(memory_space=pltpu.VMEM)
    return tuple(
        pl.pallas_call(
            functools.partial(cycle_kernel, (gx_n, gy_n, gz_n, nx, ny, depth, levels)),
            out_shape=[jax.ShapeDtypeStruct(right_side.shape, jnp.float32)] * 2,
            in_specs=[
                in_vmem,
                in_vmem,
                pl.BlockSpec(memory_space=pltpu.SMEM),
                in_vmem,
            ],
            out_specs=[in_vmem, in_vmem],
            scratch_shapes=scratch,
            compiler_params=pltpu.CompilerParams(
                collective_id=0, has_side_effects=True, vmem_limit_bytes=60 * 1024 * 1024
            ),
        )(right_side, z_faces.reshape(1, -1), xy_coupling, block_inverse)
    )


def solution(mesh):
    def call(right_side, z_faces, xy_coupling, block_inverse):
        local = body
        if fits(mesh, right_side.shape, block_inverse.shape):
            local = functools.partial(fused_body, mesh)
        return jax.shard_map(
            local,
            mesh=mesh,
            in_specs=(P("gx", "gy", "gz"), P("gz"), P(), P(None, "gz", None)),
            out_specs=(P("gx", "gy", "gz"), P("gx", "gy", "gz")),
            check_vma=False,
        )(right_side, z_faces, xy_coupling, block_inverse)

    return call
```

profile of v0, /device:TPU:0, one launch (start us, length us, event | category | flops | bytes accessed | tf_op | source)
XLA Modules:
  0.0 51.4 jit_solution(8312900526470063194)
XLA Ops:
  0.6 48.0 %shard_map.59 = (f32[32,32,128]{2,1,0:T(8,128)}, f32[32,32,128]{2,1,0:T(8,128)}) custom-call(f32[32,32,128]{2,1,0:T(8,128)} %f_ref.1, f32[1,128]{1,0:T(1,128)} %bitcast.1, f32[5]{0:T(128)} %e_ref.1, f32[5,128,128]{2,1,0:T(8,128)} %g_ref.1), custom_call_target="tpu_custom_call" | custom-call | tf_op jit(solution)/shard_map/pallas_call | solution.py:816
  48.6 0.0 copy-start
  48.6 1.9 %copy.8 = f32[32,32,128]{2,1,0:T(8,128)} copy(f32[32,32,128]{2,1,0:T(8,128)} %get-tuple-element.4) | data formatting | bytes 1048576
  50.6 0.0 copy-done
  50.6 0.8 %copy.9 = f32[32,32,128]{2,1,0:T(8,128)} copy(f32[32,32,128]{2,1,0:T(8,128)S(1)} %copy-done) | data formatting | bytes 1048576
Async XLA Ops:
  48.6 1.9 %copy-start = (f32[32,32,128]{2,1,0:T(8,128)S(1)}, f32[32,32,128]{2,1,0:T(8,128)}, u32[]{:S(2)}) copy-start(f32[32,32,128]{2,1,0:T(8,128)} %get-tuple-element.5) | copy-start | bytes 1572868
where the time goes:
time: 51.5 us; the launch traced here: 51.4 us
  Pallas kernels  48 us (93%)
  local copies, waits for them, and re-layouts  2.72 us (5%)
  between operations  0.65 us (1%)
    pallas_call x1, Pallas kernels, fused_body(): pl.pallas_call(functools.partial(cycle_kernel, (gx_n, gy_n, gz_n, nx, ny,...  48 us
    unnamed x4, local copies, waits for them, and re-layouts  2.72 us

commit v1 on v0

v1 whole, which is shorter than its diff:
```python
import functools

import jax
import jax.numpy as jnp
from jax import lax
from jax.experimental import pallas as pl
from jax.experimental.pallas import tpu as pltpu
from jax.sharding import PartitionSpec as P

LEVELS = 5
SWEEPS = 2


damping = 0.8
highest = lax.Precision.HIGHEST


def extended(cells, sides, width):
    for axis, dim in sides:
        count = lax.axis_size(axis)
        ends = count - 1
        head = lax.slice_in_dim(cells, 0, width, axis=dim)
        tail = lax.slice_in_dim(cells, cells.shape[dim] - width, cells.shape[dim], axis=dim)
        cells = jnp.concatenate(
            [
                lax.ppermute(tail, axis, [(i, (i + 1) % count) for i in range(ends)]),
                cells,
                lax.ppermute(head, axis, [((i + 1) % count, i) for i in range(ends)]),
            ],
            axis=dim,
        )
    return cells


def interface_setup(corner_aa, corner_ab, corner_ba, corner_bb, couplings):
    determinant = corner_aa * corner_bb - corner_ab * corner_ba
    corner_inverse = (
        jnp.stack(
            [jnp.stack([corner_bb, -corner_ab], -1), jnp.stack([-corner_ba, corner_aa], -1)], -2
        )
        / determinant[:, None, None]
    )
    blocks_count = corner_aa.shape[0]
    identity = jnp.eye(blocks_count, dtype=corner_inverse.dtype)
    diagonal_part = jnp.einsum("kab,kl->kalb", corner_inverse, identity, precision=highest).reshape(
        2 * blocks_count, 2 * blocks_count
    )
    link_values = jnp.zeros((2 * blocks_count - 1,), corner_inverse.dtype).at[1::2].set(-couplings)
    schur_matrix = diagonal_part + jnp.diag(link_values, 1) + jnp.diag(link_values, -1)
    return (corner_inverse, diagonal_part, jnp.linalg.cholesky(schur_matrix))


def make_solver(inverse_block, corner_rows, couplings, device_index, down_coupling, up_coupling):
    corner_inverse, diagonal_part, factor = interface_setup(
        corner_rows[:, 0], corner_rows[:, 1], corner_rows[:, 2], corner_rows[:, 3], couplings
    )
    block_len = inverse_block.shape[0]
    forward = lax.linalg.triangular_solve(factor, diagonal_part, left_side=True, lower=True)
    reach = lax.linalg.triangular_solve(
        factor, forward, left_side=True, lower=True, transpose_a=True
    )
    padded_reach = jnp.pad(reach, ((1, 1), (0, 0)))
    slice_rows = lax.dynamic_slice_in_dim(padded_reach, 2 * device_index, 4, 0)
    needed = jnp.stack([slice_rows[0], slice_rows[3]])

    def neighbours(end_values):
        zero_carry = jnp.zeros(end_values.shape, jnp.float32)
        nearby = zero_carry + jnp.dot(
            needed, lax.all_gather(end_values, "gz", axis=0, tiled=True), precision=highest
        )
        return (nearby[0], nearby[1])

    def solve(source):
        first_extent, second_extent, depth = source.shape
        line_count = first_extent * second_extent
        local_part = jnp.einsum("xyj,ij->xyi", source, inverse_block, precision=highest)
        end_values = jnp.stack(
            [
                local_part[:, :, 0].reshape(line_count),
                local_part[:, :, block_len - 1].reshape(line_count),
            ]
        )
        below_last, above_first = neighbours(end_values)
        return (
            local_part
            + (down_coupling * below_last).reshape(first_extent, second_extent, 1)
            * inverse_block[:, 0]
            + (up_coupling * above_first).reshape(first_extent, second_extent, 1)
            * inverse_block[:, block_len - 1]
        )

    return solve


def apply_operator(iterate, lateral_weight, down_faces, up_faces):
    padded = extended(iterate, (("gx", 0), ("gy", 1), ("gz", 2)), 1)
    lateral = (
        padded[:-2, 1:-1, 1:-1]
        + padded[2:, 1:-1, 1:-1]
        + padded[1:-1, :-2, 1:-1]
        + padded[1:-1, 2:, 1:-1]
    )
    return (
        lateral_weight * (4.0 * iterate - lateral)
        + down_faces * (iterate - padded[1:-1, 1:-1, :-2])
        + up_faces * (iterate - padded[1:-1, 1:-1, 2:])
    )


def restrict(field):
    first_extent, second_extent, depth = field.shape
    return field.reshape(first_extent // 2, 2, second_extent // 2, 2, depth).sum(axis=(1, 3)) * 0.25


def prolong(padded):
    first_extent = padded.shape[0] - 2
    second_extent = padded.shape[1] - 2
    depth = padded.shape[2]
    even_rows = 0.75 * padded[1:-1] + 0.25 * padded[:-2]
    odd_rows = 0.75 * padded[1:-1] + 0.25 * padded[2:]
    widened = jnp.stack([even_rows, odd_rows], 1).reshape(
        2 * first_extent, second_extent + 2, depth
    )
    even_rows = 0.75 * widened[:, 1:-1] + 0.25 * widened[:, :-2]
    odd_rows = 0.75 * widened[:, 1:-1] + 0.25 * widened[:, 2:]
    return jnp.stack([even_rows, odd_rows], 2).reshape(2 * first_extent, 2 * second_extent, depth)


def body(right_side, z_faces, xy_coupling, block_inverse):
    device_index = lax.axis_index("gz")
    levels_count = block_inverse.shape[0]
    last_cell = block_inverse.shape[1] - 1
    corner = jnp.stack(
        [
            block_inverse[:, 0, 0],
            block_inverse[:, 0, last_cell],
            block_inverse[:, last_cell, 0],
            block_inverse[:, last_cell, last_cell],
        ],
        -1,
    )[None]
    corners, firsts = (
        lax.all_gather(corner, "gz", axis=0, tiled=True),
        lax.all_gather(z_faces[:1], "gz", axis=0, tiled=True),
    )
    couplings = firsts[1:]
    edge_faces = jnp.concatenate([firsts, jnp.ones((1,), jnp.float32)])
    top_face = lax.dynamic_slice_in_dim(edge_faces, device_index + 1, 1, 0)
    up_faces = jnp.concatenate([z_faces[1:], top_face])
    solvers = [
        make_solver(
            block_inverse[level],
            corners[:, level],
            couplings,
            device_index,
            z_faces[0],
            top_face[0],
        )
        for level in range(levels_count)
    ]

    def operator(iterate, level):
        return apply_operator(iterate, xy_coupling[level], z_faces, up_faces)

    def multigrid_cycle(source, level):
        iterate = damping * solvers[level](source)
        iterate = iterate + damping * solvers[level](source - operator(iterate, level))
        if level == LEVELS - 1:
            return iterate
        coarse = multigrid_cycle(restrict(source - operator(iterate, level)), level + 1)
        widened = extended(coarse, (("gx", 0), ("gy", 1)), 1)
        iterate = iterate + prolong(widened)
        for sweep in range(SWEEPS):
            iterate = iterate + damping * solvers[level](source - operator(iterate, level))
        return iterate

    solution = multigrid_cycle(right_side, 0)
    return (solution, right_side - operator(solution, 0))


MESH = pl.DeviceIdType.MESH
HALOS = (4, 6, 6)
ROWS = (4, 5, 6)
YPAD = 8
SPARE = 32
DEEPEST = 3


def block_range(offset, own, halo, extent):
    start = offset * own - halo
    low = max(0, start)
    high = min(extent, (offset + 1) * own + halo)
    return low, high - low, low - start


def round_up(value, unit):
    return -(-value // unit) * unit


def split_planes(count, rows):
    return max(c for c in range(1, count + 1) if count % c == 0 and c * rows <= 448)


def cycle_kernel(geometry, f_hbm, z_hbm, e_hbm, g_hbm, sol_ref, res_ref, *scratch):
    gx_n, gy_n, gz_n, nx, ny, depth, levels = geometry
    refs = iter(scratch)
    take = lambda count: [next(refs) for _ in range(count)]
    sinv, g_all, z_all, gather, f_v, e_ref = take(6)
    X = [take(4) for _ in range(DEEPEST + 1)]
    X.append(take(2))
    C = take(DEEPEST + 1)
    E = take(DEEPEST + 1)
    (U1, G1, U2, G2, c3u, c3g, c4u, c4g, cwu, cwg) = take(10)
    UP, GP = [None, U1, U2, c3u, c4u], [None, G1, G2, c3g, c4g]
    OWN = [None] + take(DEEPEST)
    (in_sem, g_send, g_recv, h_send, h_recv, y_send, y_recv) = take(7)
    (x_send, x_recv, o_send, o_recv) = take(4)

    ix, iy, iz = lax.axis_index("gx"), lax.axis_index("gy"), lax.axis_index("gz")
    bx = ix * gz_n + iz
    bx_n = gx_n * gz_n
    f32 = jnp.float32

    def owned(level):
        return nx >> level, ny >> level

    def copy(src, dst, send, recv, device):
        return pltpu.make_async_remote_copy(
            src_ref=src,
            dst_ref=dst,
            send_sem=send,
            recv_sem=recv,
            device_id=device,
            device_id_type=MESH,
        )

    def inside(x, y):
        return (x >= 0) & (x < gx_n) & (y >= 0) & (y < gy_n)

    reach_all = max(
        gz_n - 1 - (-HALOS[0] // nx), *[-(-HALOS[k] // owned(k)[0]) for k in (1, 2)]
    )
    barrier = pltpu.get_barrier_semaphore()
    partners = jnp.int32(0)
    for dx in range(1 - bx_n, bx_n):
        for dy in range(1 - gy_n, gy_n):
            close = abs(dx) <= reach_all and abs(dy) <= 1
            if (dx == 0 and dy == 0) or not (close or dx == 0 or dy == 0):
                continue
            x, y = bx + dx, iy + dy
            ok = (x >= 0) & (x < bx_n) & (y >= 0) & (y < gy_n)

            @pl.when(ok)
            def _():
                pl.semaphore_signal(
                    barrier,
                    inc=1,
                    device_id=(x // gz_n, y, lax.rem(x, gz_n)),
                    device_id_type=MESH,
                )

            partners = partners + jnp.where(ok, 1, 0).astype(jnp.int32)

    parts = 4
    span = f_v.shape[0] // parts
    loads = [
        pltpu.make_async_copy(
            f_hbm.at[pl.ds(i * span, span)], f_v.at[pl.ds(i * span, span)], in_sem.at[i]
        )
        for i in range(parts)
    ]
    loads_g = [
        pltpu.make_async_copy(g_hbm.at[k], g_all.at[k, iz], in_sem.at[parts + k])
        for k in range(levels)
    ]
    loads_g.append(pltpu.make_async_copy(z_hbm, z_all.at[iz], in_sem.at[parts + levels]))
    loads_g.append(pltpu.make_async_copy(e_hbm, e_ref, in_sem.at[parts + levels + 2]))
    for c in loads:
        c.start()
    for c in loads_g:
        c.start()

    def setup_copies(other):
        here = (ix, iy, lax.rem(iz + other, gz_n))
        out = []
        for level in range(levels):
            block = g_all.at[level, iz]
            out.append(
                copy(block, block, g_send.at[other, level], g_recv.at[other, level], here)
            )
        face = z_all.at[iz]
        out.append(copy(face, face, g_send.at[other, levels], g_recv.at[other, levels], here))
        return out

    def start_copies():
        out = []
        reach = -(-HALOS[0] // nx)
        for t in range(-reach, gz_n + reach):
            xs, xn, xd = block_range(t, nx, HALOS[0], nx * gz_n)
            dgx, target = t // gz_n, t % gz_n
            for dy in (-1, 0, 1):
                ys, yn, yd = block_range(dy, ny, ROWS[0], ny)
                yd += YPAD - ROWS[0]
                out.append((t, dgx, target, dy, (xs, xn, xd), (ys, yn, yd)))
        return out

    plan0 = start_copies()
    R0 = X[0][0]
    local0 = []
    for entry in plan0:
        t, dgx, target, dy, (xs, xn, xd), (ys, yn, yd) = entry
        if dgx == 0 and dy == 0:
            move = pltpu.make_async_copy(
                f_hbm.at[pl.ds(xs, xn)],
                R0.at[pl.ds(xd, xn), target, pl.ds(yd, yn), :],
                in_sem.at[parts + levels + 1],
            )
            local0.append((target, move))

    for target, move in local0:

        @pl.when(iz == target)
        def _():
            move.start()

    def copy0(entry, source_z, device):
        t, dgx, target, dy, (xs, xn, xd), (ys, yn, yd) = entry
        slot = (t + gz_n) * 3 + dy + 1
        return copy(
            f_v.at[pl.ds(xs, xn), pl.ds(ys, yn), :],
            R0.at[pl.ds(xd, xn), source_z, pl.ds(yd, yn), :],
            h_send.at[0, slot],
            h_recv.at[0, slot, source_z],
            device,
        )

    def send0(start):
        for entry in plan0:
            t, dgx, target, dy = entry[:4]
            ok = inside(ix + dgx, iy + dy)
            if dgx == 0 and dy == 0:
                ok = ok & (iz != target)

            @pl.when(ok)
            def _():
                c = copy0(entry, iz, (ix + dgx, iy + dy, target))
                c.start() if start else c.wait_send()

    def recv0():
        for entry in plan0:
            t, dgx, target, dy = entry[:4]
            for source_z in range(gz_n):
                if dgx == 0 and dy == 0 and source_z == target:
                    continue

                @pl.when((iz == target) & inside(ix - dgx, iy - dy))
                def _():
                    copy0(entry, source_z, (ix - dgx, iy - dy, source_z)).wait_recv()

    for c in loads:
        c.wait()
    pl.semaphore_wait(barrier, partners)
    send0(True)
    for c in loads_g:
        c.wait()
    for other in range(1, gz_n):
        for c in setup_copies(other):
            c.start()

    def clear_edges():
        for level in range(DEEPEST):
            window = X[level][0]
            planes, zb, rows, lanes = window.shape
            halo = HALOS[level]
            n0, n1 = owned(level)
            reach = -(-halo // n0)
            for t in range(1, reach + 1):
                low = max(0, halo - t * n0)
                high = halo - (t - 1) * n0
                plane = jnp.zeros((high - low, zb, n1 + 2 * YPAD, lanes), f32)

                @pl.when(bx - t < 0)
                def _():
                    window[low:high, :, pl.ds(0, n1 + 2 * YPAD)] = plane

                low2, high2 = planes - high, planes - low

                @pl.when(bx + t >= bx_n)
                def _():
                    window[low2:high2, :, pl.ds(0, n1 + 2 * YPAD)] = plane

            edge = jnp.zeros((zb, YPAD, lanes), f32)

            @pl.when(iy == 0)
            def _():
                lax.fori_loop(0, planes, lambda i, c: zero_rows(window, i, 0, edge), 0)

            @pl.when(iy == gy_n - 1)
            def _():
                lax.fori_loop(
                    0, planes, lambda i, c: zero_rows(window, i, YPAD + n1, edge), 0
                )

    def fill(ref):
        zero = jnp.zeros(ref.shape[1:], f32)

        def step(i, _):
            ref[i] = zero
            return 0

        lax.fori_loop(0, ref.shape[0], step, 0)

    def clear_coarse():
        for ref in (*X[3][:3], C[3], X[4][0], c3u, c3g, c4u, c4g):
            fill(ref)

    def assemble(level, _):
        merged = g_all[level, 0]
        for k in range(1, gz_n):
            block = g_all[level, k]
            size, cz = merged.shape[0], block.shape[0]
            face = z_all[k][:, 0:1]
            a, d = block[0:1, 0:1], merged[size - 1 : size, size - 1 : size]
            last, first = merged[size - 1 : size], block[0:1]
            scale = face / (1.0 - face * face * a * d)
            p_row = jnp.concatenate([face * a * last, first], 1) * scale
            q_row = jnp.concatenate([last, face * d * first], 1) * scale
            top = jnp.concatenate([merged, jnp.zeros((size, cz), f32)], 1)
            low = jnp.concatenate([jnp.zeros((cz, size), f32), block], 1)
            top = top + merged[:, size - 1 : size] * p_row
            low = low + block[:, 0:1] * q_row
            merged = jnp.concatenate([top, low], 0)
        sinv[level] = (damping * merged).astype(jnp.bfloat16)
        return 0

    def plane_mask(level, i):
        n0 = owned(level)[0]
        x = bx * n0 - HALOS[level] + i
        return jnp.where((x >= 0) & (x < bx_n * n0), 1.0, 0.0).astype(f32)

    def row_mask(level, first, rows, stride):
        n1 = owned(level)[1]
        y = lax.broadcasted_iota(jnp.int32, (rows, depth), 0) * stride + first
        y = y + iy * n1 - YPAD
        return jnp.where((y >= 0) & (y < gy_n * n1), 1.0, 0.0).astype(f32)

    def region(level, shrink):
        if level < DEEPEST:
            n0, n1 = owned(level)
            h = ROWS[level] - shrink
            return HALOS[level] - h, n0 + 2 * h, YPAD - h, round_up(n1 + 2 * h, 8)
        window = X[level][0].shape
        return 1, window[0] - 2, YPAD, window[2] - 2 * YPAD

    def weights(level, p, c, r0, rows):
        e = e_ref[level]
        if level >= DEEPEST:
            return e
        mask = row_mask(level, r0, rows, 1)
        return jnp.stack([mask * (e * plane_mask(level, p + i)) for i in range(c)])

    def chunks(where):
        p0, planes, r0, rows = where
        c = split_planes(planes, rows)
        return [(p0 + s * c, c, r0, rows) for s in range(planes // c)]

    def around(src, k, p, c, r0, rows):
        at = lambda dp, dr: src[pl.ds(p + dp, c), k, pl.ds(r0 + dr, rows)]
        return (at(-1, 0) + at(1, 0)) + (at(0, -1) + at(0, 1))

    def line_solve(level, fields):
        flat = [v.reshape(-1, depth) for v in fields]
        lhs = jnp.concatenate(flat, 1).astype(jnp.bfloat16)
        out = jnp.dot(lhs, sinv[level], preferred_element_type=f32)
        shape = fields[0].shape
        return [out[:, k * depth : (k + 1) * depth].reshape(shape) for k in range(len(flat))]

    def relax(level, src, dst, where, place=None):
        for p, c, r0, rows in chunks(where):
            w = weights(level, p, c, r0, rows)
            total = [around(src, k, p, c, r0, rows) * w for k in range(gz_n)]
            out = line_solve(level, total)
            for k in range(gz_n):
                value = (1.0 - damping) * src[pl.ds(p, c), k, pl.ds(r0, rows)] + out[k]
                if place is None:
                    dst[pl.ds(p, c), k, pl.ds(r0, rows)] = value
                else:
                    dst[k, pl.ds(place + p - where[0], c)] = value

    def collect(level, where, place=None, offset=0):
        for p, c, r0, rows in chunks(where):
            at = lambda ref, k: ref[pl.ds(p, c), k, pl.ds(r0, rows)]
            total = []
            for k in range(gz_n):
                part = [at(ref, k) for ref in X[level]]
                while len(part) > 1:
                    part = [part[i] + part[i + 1] for i in range(0, len(part), 2)]
                total.append(part[0])
            out = line_solve(level, total)
            for k in range(gz_n):
                u = out[k] if level > DEEPEST else out[k] + at(C[level], k)
                if level == 0:
                    sol_ref[k, pl.ds(place + p - where[0], c)] = u
                    continue
                g = damping * total[k] + (4.0 * (e_ref[level - 1] - e_ref[level])) * u
                if level <= DEEPEST:
                    g = g + at(E[level], k)
                UP[level][pl.ds(p + offset, c), k, pl.ds(r0, rows)] = u
                GP[level][pl.ds(p + offset, c), k, pl.ds(r0, rows)] = g

    def restrict_planes(level, dst, planes, x0, y0, to_plane, to_row, rows):
        src = X[level][2]
        for j in range(planes):
            for k in range(gz_n):
                total = None
                for a in (0, 1):
                    for b in (0, 1):
                        part = src[x0 + 2 * j + a, k, pl.ds(y0 + b, rows, 2), :]
                        total = part if total is None else total + part
                dst[to_plane + j, k, pl.ds(to_row, rows), :] = total * 0.25

    def prolong(level, x0, y0, coarse):
        shift = 1 if level >= DEEPEST else 0
        p0, planes, r0, rows = region(level, 1)
        low, high = p0 - shift, p0 - shift + planes
        first = r0 // 2 * 2
        half = round_up((r0 + rows - first + 1) // 2, 8) if level < DEEPEST else rows // 2
        start = y0 + (first // 2 if level < DEEPEST else 0)
        masks = [
            row_mask(level, first + b, half, 2) if level < DEEPEST else None for b in (0, 1)
        ]
        mixes = {}

        def mixed(src, index, j, k):
            key = (index, j, k)
            if key not in mixes:
                load = lambda dy: src[x0 + j, k, pl.ds(start + dy, half), :]
                quarter = 0.25 * load(0)
                near = load(0) - quarter
                out = []
                for dy in (-1, 1):
                    value = near + 0.25 * load(dy)
                    far = 0.25 * value
                    out.append((value - far, far))
                mixes[key] = out
            return mixes[key]

        for j in range(low // 2, (high - 1) // 2 + 1):
            for a in (0, 1):
                p = 2 * j + a
                if not low <= p < high:
                    continue
                for b in (0, 1):
                    if level < DEEPEST:
                        mask = masks[b] * plane_mask(level, p)
                    for index, (src, dst) in enumerate(coarse):
                        for k in range(gz_n):
                            near = mixed(src, index, j, k)[b][0]
                            value = near + mixed(src, index, j + 2 * a - 1, k)[b][1]
                            if level < DEEPEST:
                                value = value * mask
                            dst[p + shift, k, pl.ds(first + b, half, 2), :] = value

    def correct(level, coarse_u, coarse_g, x0, y0):
        prolong(level, x0, y0, [(coarse_u, C[level]), (coarse_g, E[level])])
        where = region(level, 2)
        target = X[level][2]
        for p, c, r0, rows in chunks(where):
            w = weights(level, p, c, r0, rows)
            for k in range(gz_n):
                at = lambda ref: ref[pl.ds(p, c), k, pl.ds(r0, rows)]
                total = around(C[level], k, p, c, r0, rows) * w
                target[pl.ds(p, c), k, pl.ds(r0, rows)] = at(target) + (total - at(E[level]))

    def exchange(level, meanwhile):
        n0, n1 = owned(level)
        halo = HALOS[level]
        own = OWN[level]
        reach = -(-halo // n0)
        window = X[level][0]

        def each(act):
            slot = 0
            for t in range(-reach, reach + 1):
                xs, xn, xd = block_range(t, n0, halo, n0)
                for dy in (-1, 0, 1):
                    if t == 0 and dy == 0:
                        continue
                    ys, yn, yd = block_range(dy, n1, ROWS[level], n1)
                    yd += YPAD - ROWS[level]
                    act(t, dy, (xs, xn, xd), (ys, yn, yd), slot)
                    slot += 1

        def build(t, dy, x, y, slot):
            there = bx + t + bx_n
            return copy(
                own.at[pl.ds(x[0], x[1]), :, pl.ds(y[0], y[1]), :],
                window.at[pl.ds(x[2], x[1]), :, pl.ds(y[2], y[1]), :],
                h_send.at[level, slot],
                h_recv.at[level, slot, 0],
                (there // gz_n - gx_n, iy + dy, lax.rem(there, gz_n)),
            )

        def valid(x, y):
            return (x >= 0) & (x < bx_n) & (y >= 0) & (y < gy_n)

        def start(t, dy, x, y, slot):
            @pl.when(valid(bx + t, iy + dy))
            def _():
                build(t, dy, x, y, slot).start()

        def finish(t, dy, x, y, slot):
            @pl.when(valid(bx - t, iy - dy))
            def _():
                build(t, dy, x, y, slot).wait_recv()

        def drain(t, dy, x, y, slot):
            @pl.when(valid(bx + t, iy + dy))
            def _():
                build(t, dy, x, y, slot).wait_send()

        each(start)
        for i in range(n0):
            window[i + halo, :, pl.ds(YPAD, n1), :] = own[i]
        meanwhile()
        each(finish)
        return lambda: each(drain)

    def gather_all():
        own3 = OWN[3]

        def line_y(other, slot):
            return copy(
                own3,
                gather.at[bx, slot],
                y_send.at[other],
                y_recv.at[slot],
                (ix, other, iz),
            )

        def line_x(src, other, slot_x, slot_y):
            return copy(
                src,
                gather.at[slot_x, slot_y],
                x_send.at[other, slot_y],
                x_recv.at[slot_x, slot_y],
                (other // gz_n, iy, lax.rem(other, gz_n)),
            )

        def others(me, count, act):
            for s in range(1, count):
                act(lax.rem(me + s, count))

        others(iy, gy_n, lambda y: line_y(y, iy).start())
        others(bx, bx_n, lambda x: line_x(own3, x, bx, iy).start())
        gather[bx, iy] = own3[...]
        for distance in range(1, gy_n):
            for y in (iy + distance, iy - distance):

                @pl.when((y >= 0) & (y < gy_n))
                def _():
                    line_y(y, y).wait_recv()
                    block = gather.at[bx, y]
                    others(bx, bx_n, lambda x: line_x(block, x, bx, y).start())

        def arrive(x):
            for y in range(gy_n):
                line_x(own3, x, x, y).wait_recv()

        others(bx, bx_n, arrive)
        n0, n1 = owned(3)
        window = X[3][0]

        def place(b, _):
            for i in range(n0):
                for y in range(gy_n):
                    window[1 + b * n0 + i, :, pl.ds(YPAD + y * n1, n1), :] = gather[b, y, i]
            return 0

        lax.fori_loop(0, bx_n, place, 0)

        def drains():
            others(iy, gy_n, lambda y: line_y(y, iy).wait_send())

            def leave(x):
                for y in range(gy_n):
                    line_x(own3, x, bx, y).wait_send()

            others(bx, bx_n, leave)

        return drains

    clear_edges()
    for other in range(1, gz_n):
        for c in setup_copies(other):
            c.wait()
    assemble(0, 0)
    for target, move in local0:

        @pl.when(iz == target)
        def _():
            move.wait()

    recv0()
    drains = [lambda: send0(False)]

    def later():
        lax.fori_loop(1, levels, assemble, 0)

    for level in range(DEEPEST):
        one, two = X[level][1], X[level][2]
        relax(level, X[level][0], one, region(level, 1))
        relax(level, one, two, region(level, 2))
        n0, n1 = owned(level + 1)
        restrict_planes(level, OWN[level + 1], n0, HALOS[level], YPAD, 0, 0, n1)
        if level < DEEPEST - 1:
            drains.append(exchange(level + 1, (later, clear_coarse)[level]))
        else:
            drains.append(gather_all())

    whole3, whole4 = region(3, 0), region(4, 0)
    relax(3, X[3][0], X[3][1], whole3)
    relax(3, X[3][1], X[3][2], whole3)
    restrict_planes(3, X[4][0], whole4[1], 1, YPAD, 1, YPAD, whole4[3])
    relax(4, X[4][0], X[4][1], whole4)
    collect(4, whole4)
    correct(3, c4u, c4g, 1, YPAD)
    relax(3, X[3][2], X[3][3], whole3)
    pad3 = HALOS[2] // 2 + 1
    collect(3, whole3, offset=pad3 - 1)
    n0, n1 = owned(3)
    margin = YPAD // 2
    for y in range(gy_n):

        @pl.when(iy == y)
        def _():
            for j in range(HALOS[2] + 2 * n0):
                for src, dst in ((c3u, cwu), (c3g, cwg)):
                    dst[j, :, pl.ds(margin, n1 + 4 * margin), :] = src[
                        bx * n0 + j, :, pl.ds(y * n1, n1 + 4 * margin), :
                    ]

    for level in (2, 1, 0):
        if level == 2:
            correct(2, cwu, cwg, 1, YPAD)
        else:
            x0 = HALOS[level + 1] - HALOS[level] // 2
            correct(level, UP[level + 1], GP[level + 1], x0, YPAD // 2)
        where = region(level, 3)
        relax(level, X[level][2], X[level][3], where)
        if level:
            collect(level, where)

    def out_copies(which):
        ref = (sol_ref, res_ref)[which]
        out = []
        for other in range(1, gz_n):
            there = lax.rem(iz + other, gz_n)
            block = ref.at[there, pl.ds(iz * nx, nx)]
            out.append(
                copy(
                    block,
                    block,
                    o_send.at[which, other],
                    o_recv.at[which, other],
                    (ix, iy, there),
                )
            )
        return out

    own0 = (HALOS[0], nx, YPAD, ny)
    collect(0, own0, place=iz * nx)
    for c in out_copies(0):
        c.start()
    relax(0, X[0][3], res_ref, own0, place=iz * nx)
    for c in out_copies(1):
        c.start()
    for drain in drains:
        drain()
    for which in (0, 1):
        for c in out_copies(which):
            c.wait()


def zero_rows(ref, i, at, value):
    ref[i, :, pl.ds(at, YPAD), :] = value
    return 0


def store_kernel(pieces, sol_v, res_v, sol_hbm, res_hbm, sem):
    iz = lax.axis_index("gz")
    span = sol_hbm.shape[0] // pieces
    moves = []
    for which, (src, dst) in enumerate(((sol_v, sol_hbm), (res_v, res_hbm))):
        for i in range(pieces):
            at = pl.ds(i * span, span)
            moves.append(
                pltpu.make_async_copy(src.at[iz, at], dst.at[at], sem.at[which, i])
            )
    for move in moves:
        move.start()
    for move in moves:
        move.wait()


def fits(mesh, shape, inverse_shape):
    gx_n, gy_n, gz_n = (mesh.shape[a] for a in ("gx", "gy", "gz"))
    nx, ny = shape[0] // (gx_n * gz_n), shape[1] // gy_n
    return (
        inverse_shape[0] == LEVELS == 5
        and SWEEPS == 2
        and inverse_shape[2] == 128
        and nx % 8 == 0
        and ny % 32 == 0
        and (shape[1] >> 4) % 8 == 0
        and gz_n <= 2
    )


def fused_body(mesh, right_side, z_faces, xy_coupling, block_inverse):
    gx_n, gy_n, gz_n = (mesh.shape[a] for a in ("gx", "gy", "gz"))
    levels, _, depth = block_inverse.shape
    nx, ny = right_side.shape[0] // gz_n, right_side.shape[1]
    windows = []
    for level in range(levels):
        if level < DEEPEST:
            size = ((nx >> level) + 2 * HALOS[level], (ny >> level) + SPARE)
        else:
            size = (
                ((nx * gx_n * gz_n) >> level) + 2,
                ((ny * gy_n) >> level) + 2 * YPAD,
            )
        windows.append((size[0], gz_n, size[1], depth))
    vmem = lambda shape: pltpu.VMEM(shape, jnp.float32)
    full3, full4 = windows[3], windows[4]
    pad3 = HALOS[2] // 2 + 1
    c4 = full4
    c3 = (full3[0] - 2 + 2 * pad3,) + full3[1:]
    cw = (windows[2][0] // 2 + 2, gz_n, (ny >> 3) + 28, depth)
    reach = 2 * max(-(-HALOS[k] // (nx >> k)) for k in range(3)) + 1
    slots = 3 * max(reach, 3 * gz_n + 1)
    bx_n = gx_n * gz_n
    dma = pltpu.SemaphoreType.DMA
    own = lambda k: (nx >> k, gz_n, ny >> k, depth)
    scratch = (
        [
            pltpu.VMEM((levels, gz_n * depth, gz_n * depth), jnp.bfloat16),
            vmem((levels, gz_n, depth, depth)),
            vmem((gz_n, 1, depth)),
            vmem((bx_n, gy_n) + own(3)),
            vmem(right_side.shape),
            pltpu.SMEM((levels,), jnp.float32),
        ]
        + [vmem(w) for w in windows[: DEEPEST + 1] for _ in range(4)]
        + [vmem(full4)] * 2
        + [vmem(w) for w in windows[: DEEPEST + 1]] * 2
        + [vmem(windows[1])] * 2
        + [vmem(windows[2])] * 2
        + [vmem(c3), vmem(c3), vmem(c4), vmem(c4), vmem(cw), vmem(cw)]
        + [vmem(own(1)), vmem(own(2)), vmem(own(3))]
        + [dma((levels + 8,))]
        + [dma((gz_n, levels + 1))] * 2
        + [dma((3, slots)), dma((3, slots, gz_n))]
        + [dma((gy_n,))] * 2
        + [dma((bx_n, gy_n))] * 2
        + [dma((2, gz_n))] * 2
    )
    in_vmem = pl.BlockSpec(memory_space=pltpu.VMEM)
    in_hbm = pl.BlockSpec(memory_space=pltpu.HBM)
    staged = (gz_n,) + right_side.shape
    hold = lambda x: pltpu.with_memory_space_constraint(x, pltpu.HBM)
    halves = pl.pallas_call(
        functools.partial(cycle_kernel, (gx_n, gy_n, gz_n, nx, ny, depth, levels)),
        out_shape=[pltpu.VMEM(staged, jnp.float32)] * 2,
        in_specs=[
            in_hbm,
            in_hbm,
            in_hbm,
            in_hbm,
        ],
        out_specs=[in_vmem, in_vmem],
        scratch_shapes=scratch,
        compiler_params=pltpu.CompilerParams(
            collective_id=0, has_side_effects=True, vmem_limit_bytes=48 * 1024 * 1024
        ),
    )(hold(right_side), hold(z_faces.reshape(1, -1)), hold(xy_coupling), hold(block_inverse))
    pieces = 4
    return tuple(
        pl.pallas_call(
            functools.partial(store_kernel, pieces),
            out_shape=[jax.ShapeDtypeStruct(right_side.shape, jnp.float32)] * 2,
            in_specs=[in_vmem, in_vmem],
            out_specs=[in_hbm, in_hbm],
            scratch_shapes=[dma((2, pieces))],
        )(*[pltpu.with_memory_space_constraint(x, pltpu.VMEM) for x in halves])
    )


def solution(mesh):
    def call(right_side, z_faces, xy_coupling, block_inverse):
        local = body
        if fits(mesh, right_side.shape, block_inverse.shape):
            local = functools.partial(fused_body, mesh)
        return jax.shard_map(
            local,
            mesh=mesh,
            in_specs=(P("gx", "gy", "gz"), P("gz"), P(), P(None, "gz", None)),
            out_specs=(P("gx", "gy", "gz"), P("gx", "gy", "gz")),
            check_vma=False,
        )(right_side, z_faces, xy_coupling, block_inverse)

    return call
```

time: 51.5 us -> 38.6 us (0.75)
  Pallas kernels: 48 us -> 37.8 us
  local copies, waits for them, and re-layouts: 2.72 us -> 0 us
    pallas_call x1, Pallas kernels: 48 us -> 36.8 us  [fused_body(): pl.pallas_call(functools.partial(cycle_kernel, (gx_n, gy_n, gz_n, nx, ny,...]
    unnamed x4 -> x0, local copies, waits for them, and re-layouts: 2.72 us -> none
    pallas_call x0 -> x1, Pallas kernels: none -> 1.03 us  [fused_body(): pl.pallas_call(functools.partial(store_kernel, pieces), out_shape=[jax.Sh...]
where the time goes in v1:
time: 38.6 us; the launch traced here: 38.5 us
  Pallas kernels  37.8 us (98%)
  between operations  0.64 us (2%)
    pallas_call x1, Pallas kernels, fused_body(): pl.pallas_call(functools.partial(cycle_kernel, (gx_n, gy_n, gz_n, nx, ny,...  36.8 us
    pallas_call x1, Pallas kernels, fused_body(): pl.pallas_call(functools.partial(store_kernel, pieces), out_shape=[jax.Sh...  1.03 us

profile of v1, /device:TPU:0, one launch (start us, length us, event | category | flops | bytes accessed | tf_op | source)
XLA Modules:
  0.0 38.5 jit_solution(329188799068201755)
XLA Ops:
  0.6 36.8 %shard_map.59 = (f32[2,32,32,128]{3,2,1,0:T(8,128)S(1)}, f32[2,32,32,128]{3,2,1,0:T(8,128)S(1)}) custom-call(f32[32,32,128]{2,1,0:T(8,128)} %f_hbm.1, f32[1,128]{1,0:T(1,128)} %bitcast.1, f32[5]{0:T(128)} %e_hbm.1, f32[5,128,128]{2,1,0:T(8,128)} %g_hbm.1), custom_call_target="tpu_custom_call" | custom-call | tf_op jit(solution)/shard_map/pallas_call | solution.py:872
  37.5 1.0 %shard_map.60 = (f32[32,32,128]{2,1,0:T(8,128)}, f32[32,32,128]{2,1,0:T(8,128)}) custom-call(f32[2,32,32,128]{3,2,1,0:T(8,128)S(1)} %get-tuple-element.4.sol_v, f32[2,32,32,128]{3,2,1,0:T(8,128)S(1)} %get-tuple-element.5.res_v), custom_call_target="tpu_custom_call" | custom-call | tf_op jit(solution)/shard_map/pallas_call | solution.py:889

commit v2 on v1

--- a/solution.py
+++ b/solution.py
@@ -212,9 +212,9 @@
     E = take(DEEPEST + 1)
     (U1, G1, U2, G2, c3u, c3g, c4u, c4g, cwu, cwg) = take(10)
     UP, GP = [None, U1, U2, c3u, c4u], [None, G1, G2, c3g, c4g]
-    OWN = [None] + take(DEEPEST)
-    (in_sem, g_send, g_recv, h_send, h_recv, y_send, y_recv) = take(7)
-    (x_send, x_recv, o_send, o_recv) = take(4)
+    own3, pool = take(2)
+    (in_sem, g_send, g_recv, h_send, h_recv, y_recv, p_sem) = take(7)
+    y_send, x_send, x_recv, o_send, o_recv = [p_sem.at[i] for i in range(5)]
 
     ix, iy, iz = lax.axis_index("gx"), lax.axis_index("gy"), lax.axis_index("gz")
     bx = ix * gz_n + iz
@@ -237,6 +237,22 @@
     def inside(x, y):
         return (x >= 0) & (x < gx_n) & (y >= 0) & (y < gy_n)
 
+    parts = 4
+    span = f_v.shape[0] // parts
+    for i in range(parts):
+        at = pl.ds(i * span, span)
+        pltpu.make_async_copy(f_hbm.at[at], f_v.at[at], in_sem.at[0]).start()
+    f_load = pltpu.make_async_copy(f_hbm, f_v, in_sem.at[0])
+    rest = pl.ds(1, levels - 1)
+    loads = [
+        pltpu.make_async_copy(z_hbm, z_all.at[iz], in_sem.at[1]),
+        pltpu.make_async_copy(g_hbm.at[0], g_all.at[0, iz], in_sem.at[2]),
+        pltpu.make_async_copy(g_hbm.at[rest], g_all.at[rest, iz], in_sem.at[3]),
+        pltpu.make_async_copy(e_hbm, e_ref, in_sem.at[4]),
+    ]
+    for c in loads:
+        c.start()
+
     reach_all = max(
         gz_n - 1 - (-HALOS[0] // nx), *[-(-HALOS[k] // owned(k)[0]) for k in (1, 2)]
     )
@@ -261,36 +277,34 @@
 
             partners = partners + jnp.where(ok, 1, 0).astype(jnp.int32)
 
-    parts = 4
-    span = f_v.shape[0] // parts
-    loads = [
-        pltpu.make_async_copy(
-            f_hbm.at[pl.ds(i * span, span)], f_v.at[pl.ds(i * span, span)], in_sem.at[i]
-        )
-        for i in range(parts)
-    ]
-    loads_g = [
-        pltpu.make_async_copy(g_hbm.at[k], g_all.at[k, iz], in_sem.at[parts + k])
-        for k in range(levels)
-    ]
-    loads_g.append(pltpu.make_async_copy(z_hbm, z_all.at[iz], in_sem.at[parts + levels]))
-    loads_g.append(pltpu.make_async_copy(e_hbm, e_ref, in_sem.at[parts + levels + 2]))
-    for c in loads:
-        c.start()
-    for c in loads_g:
-        c.start()
-
     def setup_copies(other):
         here = (ix, iy, lax.rem(iz + other, gz_n))
         out = []
-        for level in range(levels):
-            block = g_all.at[level, iz]
-            out.append(
-                copy(block, block, g_send.at[other, level], g_recv.at[other, level], here)
-            )
-        face = z_all.at[iz]
-        out.append(copy(face, face, g_send.at[other, levels], g_recv.at[other, levels], here))
+        for i, block in enumerate((z_all.at[iz], g_all.at[0, iz], g_all.at[rest, iz])):
+            out.append(copy(block, block, g_send.at[other, i], g_recv.at[other, i], here))
         return out
+
+    def runs(count, key):
+        out = []
+        for i in range(count):
+            if out and key(i) == out[-1][2]:
+                out[-1][1] = i
+            else:
+                out.append([i, i, key(i)])
+        return [(low, high) for low, high, _ in out]
+
+    def take_rows(sem, rows):
+        block = pool.at[pl.ds(0, rows)]
+        pltpu.make_async_copy(block, block, sem).wait()
+
+    def settle(sem, total):
+        table = [[total(b, y) for y in range(gy_n)] for b in range(bx_n)]
+        for low, high in runs(bx_n, lambda b: table[b]):
+            for first, last in runs(gy_n, lambda y: [row[y] for row in table]):
+
+                @pl.when((bx >= low) & (bx <= high) & (iy >= first) & (iy <= last))
+                def _():
+                    take_rows(sem, table[low][first])
 
     def start_copies():
         out = []
@@ -313,7 +327,7 @@
             move = pltpu.make_async_copy(
                 f_hbm.at[pl.ds(xs, xn)],
                 R0.at[pl.ds(xd, xn), target, pl.ds(yd, yn), :],
-                in_sem.at[parts + levels + 1],
+                in_sem.at[5],
             )
             local0.append((target, move))
 
@@ -325,16 +339,15 @@
 
     def copy0(entry, source_z, device):
         t, dgx, target, dy, (xs, xn, xd), (ys, yn, yd) = entry
-        slot = (t + gz_n) * 3 + dy + 1
         return copy(
             f_v.at[pl.ds(xs, xn), pl.ds(ys, yn), :],
             R0.at[pl.ds(xd, xn), source_z, pl.ds(yd, yn), :],
-            h_send.at[0, slot],
-            h_recv.at[0, slot, source_z],
+            h_send.at[0],
+            h_recv.at[0],
             device,
         )
 
-    def send0(start):
+    def send0():
         for entry in plan0:
             t, dgx, target, dy = entry[:4]
             ok = inside(ix + dgx, iy + dy)
@@ -343,29 +356,27 @@
 
             @pl.when(ok)
             def _():
-                c = copy0(entry, iz, (ix + dgx, iy + dy, target))
-                c.start() if start else c.wait_send()
-
-    def recv0():
-        for entry in plan0:
-            t, dgx, target, dy = entry[:4]
+                copy0(entry, iz, (ix + dgx, iy + dy, target)).start()
+
+    def in_grid(b, y):
+        return 0 <= b < bx_n and 0 <= y < gy_n
+
+    def sent0(b, y):
+        total = 0
+        for t, dgx, target, dy, (_, xn, _), (_, yn, _) in plan0:
+            there = (b // gz_n + dgx) * gz_n + target
+            if in_grid(there, y + dy) and (there, dy) != (b, 0):
+                total += xn * yn
+        return total
+
+    def received0(b, y):
+        total = 0
+        for t, dgx, target, dy, (_, xn, _), (_, yn, _) in plan0:
             for source_z in range(gz_n):
-                if dgx == 0 and dy == 0 and source_z == target:
-                    continue
-
-                @pl.when((iz == target) & inside(ix - dgx, iy - dy))
-                def _():
-                    copy0(entry, source_z, (ix - dgx, iy - dy, source_z)).wait_recv()
-
-    for c in loads:
-        c.wait()
-    pl.semaphore_wait(barrier, partners)
-    send0(True)
-    for c in loads_g:
-        c.wait()
-    for other in range(1, gz_n):
-        for c in setup_copies(other):
-            c.start()
+                there = (b // gz_n - dgx) * gz_n + source_z
+                if target == b % gz_n and in_grid(there, y - dy) and (there, dy) != (b, 0):
+                    total += xn * yn
+        return total
 
     def clear_edges():
         for level in range(DEEPEST):
@@ -572,78 +583,66 @@
                 total = around(C[level], k, p, c, r0, rows) * w
                 target[pl.ds(p, c), k, pl.ds(r0, rows)] = at(target) + (total - at(E[level]))
 
+    def spans(own, reach, width, start):
+        out = {0: (start - 1, own + 2)}
+        near = 2
+        for t in range(1, reach + 1):
+            far = min(width, t * own + 1)
+            if far >= near:
+                out[t] = (start - far, far - near + 1)
+                out[-t] = (start + own - 1 + near, far - near + 1)
+            near = far + 1
+        return out
+
     def exchange(level, meanwhile):
         n0, n1 = owned(level)
-        halo = HALOS[level]
-        own = OWN[level]
-        reach = -(-halo // n0)
+        width = ROWS[level]
         window = X[level][0]
-
-        def each(act):
-            slot = 0
-            for t in range(-reach, reach + 1):
-                xs, xn, xd = block_range(t, n0, halo, n0)
-                for dy in (-1, 0, 1):
-                    if t == 0 and dy == 0:
-                        continue
-                    ys, yn, yd = block_range(dy, n1, ROWS[level], n1)
-                    yd += YPAD - ROWS[level]
-                    act(t, dy, (xs, xn, xd), (ys, yn, yd), slot)
-                    slot += 1
-
-        def build(t, dy, x, y, slot):
-            there = bx + t + bx_n
-            return copy(
-                own.at[pl.ds(x[0], x[1]), :, pl.ds(y[0], y[1]), :],
-                window.at[pl.ds(x[2], x[1]), :, pl.ds(y[2], y[1]), :],
-                h_send.at[level, slot],
-                h_recv.at[level, slot, 0],
-                (there // gz_n - gx_n, iy + dy, lax.rem(there, gz_n)),
-            )
+        along_x = spans(n0, -(-width // n0), width, HALOS[level])
+        along_y = spans(n1, 1, width, YPAD)
+        pieces = [(t, dy) for t in along_x for dy in along_y if t or dy]
 
         def valid(x, y):
             return (x >= 0) & (x < bx_n) & (y >= 0) & (y < gy_n)
 
-        def start(t, dy, x, y, slot):
+        for t, dy in pieces:
+            (p, planes), (r, rows) = along_x[t], along_y[dy]
+            there = bx + t + bx_n
+
             @pl.when(valid(bx + t, iy + dy))
             def _():
-                build(t, dy, x, y, slot).start()
-
-        def finish(t, dy, x, y, slot):
-            @pl.when(valid(bx - t, iy - dy))
-            def _():
-                build(t, dy, x, y, slot).wait_recv()
-
-        def drain(t, dy, x, y, slot):
-            @pl.when(valid(bx + t, iy + dy))
-            def _():
-                build(t, dy, x, y, slot).wait_send()
-
-        each(start)
-        for i in range(n0):
-            window[i + halo, :, pl.ds(YPAD, n1), :] = own[i]
+                copy(
+                    window.at[pl.ds(p + t * n0, planes), :, pl.ds(r + dy * n1, rows), :],
+                    window.at[pl.ds(p, planes), :, pl.ds(r, rows), :],
+                    h_send.at[level],
+                    h_recv.at[level],
+                    (there // gz_n - gx_n, iy + dy, lax.rem(there, gz_n)),
+                ).start()
+
+        def total(sign):
+            def count(b, y):
+                return sum(
+                    gz_n * along_x[t][1] * along_y[dy][1]
+                    for t, dy in pieces
+                    if in_grid(b + sign * t, y + sign * dy)
+                )
+
+            return count
+
         meanwhile()
-        each(finish)
-        return lambda: each(drain)
+        settle(h_recv.at[level], total(-1))
+        return lambda: settle(h_send.at[level], total(1))
 
     def gather_all():
-        own3 = OWN[3]
-
         def line_y(other, slot):
-            return copy(
-                own3,
-                gather.at[bx, slot],
-                y_send.at[other],
-                y_recv.at[slot],
-                (ix, other, iz),
-            )
+            return copy(own3, gather.at[bx, slot], y_send, y_recv.at[slot], (ix, other, iz))
 
         def line_x(src, other, slot_x, slot_y):
             return copy(
                 src,
                 gather.at[slot_x, slot_y],
-                x_send.at[other, slot_y],
-                x_recv.at[slot_x, slot_y],
+                x_send,
+                x_recv,
                 (other // gz_n, iy, lax.rem(other, gz_n)),
             )
 
@@ -663,11 +662,8 @@
                     block = gather.at[bx, y]
                     others(bx, bx_n, lambda x: line_x(block, x, bx, y).start())
 
-        def arrive(x):
-            for y in range(gy_n):
-                line_x(own3, x, x, y).wait_recv()
-
-        others(bx, bx_n, arrive)
+        size = own3.shape[0] * own3.shape[1] * own3.shape[2]
+        take_rows(x_recv, (bx_n - 1) * gy_n * size)
         n0, n1 = owned(3)
         window = X[3][0]
 
@@ -680,19 +676,23 @@
         lax.fori_loop(0, bx_n, place, 0)
 
         def drains():
-            others(iy, gy_n, lambda y: line_y(y, iy).wait_send())
-
-            def leave(x):
-                for y in range(gy_n):
-                    line_x(own3, x, bx, y).wait_send()
-
-            others(bx, bx_n, leave)
+            take_rows(y_send, (gy_n - 1) * size)
+            take_rows(x_send, (bx_n - 1) * gy_n * size)
 
         return drains
 
     clear_edges()
-    for other in range(1, gz_n):
-        for c in setup_copies(other):
+    f_load.wait()
+    pl.semaphore_wait(barrier, partners)
+    send0()
+    for c in loads:
+        c.wait()
+    setups = [setup_copies(other) for other in range(1, gz_n)]
+    for group in setups:
+        for c in group:
+            c.start()
+    for group in setups:
+        for c in group[:2]:
             c.wait()
     assemble(0, 0)
     for target, move in local0:
@@ -701,10 +701,12 @@
         def _():
             move.wait()
 
-    recv0()
-    drains = [lambda: send0(False)]
+    settle(h_recv.at[0], received0)
+    drains = [lambda: settle(h_send.at[0], sent0)]
 
     def later():
+        for group in setups:
+            group[2].wait()
         lax.fori_loop(1, levels, assemble, 0)
 
     for level in range(DEEPEST):
@@ -712,10 +714,14 @@
         relax(level, X[level][0], one, region(level, 1))
         relax(level, one, two, region(level, 2))
         n0, n1 = owned(level + 1)
-        restrict_planes(level, OWN[level + 1], n0, HALOS[level], YPAD, 0, 0, n1)
+        p, r = HALOS[level], YPAD
         if level < DEEPEST - 1:
+            to_plane = HALOS[level + 1] - 1
+            window = X[level + 1][0]
+            restrict_planes(level, window, n0 + 2, p - 2, r - 2, to_plane, YPAD - 1, n1 + 2)
             drains.append(exchange(level + 1, (later, clear_coarse)[level]))
         else:
+            restrict_planes(level, own3, n0, p, r, 0, 0, n1)
             drains.append(gather_all())
 
     whole3, whole4 = region(3, 0), region(4, 0)
@@ -751,35 +757,26 @@
         if level:
             collect(level, where)
 
-    def out_copies(which):
-        ref = (sol_ref, res_ref)[which]
-        out = []
+    def send_out(ref, p, c):
         for other in range(1, gz_n):
             there = lax.rem(iz + other, gz_n)
-            block = ref.at[there, pl.ds(iz * nx, nx)]
-            out.append(
-                copy(
-                    block,
-                    block,
-                    o_send.at[which, other],
-                    o_recv.at[which, other],
-                    (ix, iy, there),
-                )
-            )
-        return out
-
-    own0 = (HALOS[0], nx, YPAD, ny)
-    collect(0, own0, place=iz * nx)
-    for c in out_copies(0):
-        c.start()
-    relax(0, X[0][3], res_ref, own0, place=iz * nx)
-    for c in out_copies(1):
-        c.start()
+            block = ref.at[there, pl.ds(iz * nx + p, c)]
+            copy(block, block, o_send, o_recv, (ix, iy, there)).start()
+
+    quarter = nx // 4
+    own0 = [(HALOS[0] + p, quarter, YPAD, ny) for p in range(0, nx, quarter)]
+    for where in own0:
+        p = where[0] - HALOS[0]
+        collect(0, where, place=iz * nx + p)
+        send_out(sol_ref, p, quarter)
+    for where in own0:
+        p = where[0] - HALOS[0]
+        relax(0, X[0][3], res_ref, where, place=iz * nx + p)
+        send_out(res_ref, p, quarter)
     for drain in drains:
         drain()
-    for which in (0, 1):
-        for c in out_copies(which):
-            c.wait()
+    for sem in (o_send, o_recv):
+        take_rows(sem, (gz_n - 1) * 2 * nx * ny)
 
 
 def zero_rows(ref, i, at, value):
@@ -837,8 +834,7 @@
     c4 = full4
     c3 = (full3[0] - 2 + 2 * pad3,) + full3[1:]
     cw = (windows[2][0] // 2 + 2, gz_n, (ny >> 3) + 28, depth)
-    reach = 2 * max(-(-HALOS[k] // (nx >> k)) for k in range(3)) + 1
-    slots = 3 * max(reach, 3 * gz_n + 1)
+    most = gz_n * (nx + 2 * HALOS[0] + 8) * (ny + 2 * YPAD)
     bx_n = gx_n * gz_n
     dma = pltpu.SemaphoreType.DMA
     own = lambda k: (nx >> k, gz_n, ny >> k, depth)
@@ -857,13 +853,11 @@
         + [vmem(windows[1])] * 2
         + [vmem(windows[2])] * 2
         + [vmem(c3), vmem(c3), vmem(c4), vmem(c4), vmem(cw), vmem(cw)]
-        + [vmem(own(1)), vmem(own(2)), vmem(own(3))]
-        + [dma((levels + 8,))]
-        + [dma((gz_n, levels + 1))] * 2
-        + [dma((3, slots)), dma((3, slots, gz_n))]
-        + [dma((gy_n,))] * 2
-        + [dma((bx_n, gy_n))] * 2
-        + [dma((2, gz_n))] * 2
+        + [vmem(own(3)), vmem((most, depth))]
+        + [dma((6,))]
+        + [dma((gz_n, 3))] * 2
+        + [dma((DEEPEST,))] * 2
+        + [dma((gy_n,)), dma((5,))]
     )
     in_vmem = pl.BlockSpec(memory_space=pltpu.VMEM)
     in_hbm = pl.BlockSpec(memory_space=pltpu.HBM)

time: 38.6 us -> 35.5 us (0.920)
  Pallas kernels: 37.8 us -> 34.7 us
    pallas_call x1, Pallas kernels: 36.8 us -> 33.7 us  [fused_body(): pl.pallas_call(functools.partial(cycle_kernel, (gx_n, gy_n, gz_n, nx, ny,...]
where the time goes in v2:
time: 35.5 us; the launch traced here: 35.3 us
  Pallas kernels  34.7 us (98%)
  between operations  0.64 us (2%)
    pallas_call x1, Pallas kernels, fused_body(): pl.pallas_call(functools.partial(cycle_kernel, (gx_n, gy_n, gz_n, nx, ny,...  33.7 us
    pallas_call x1, Pallas kernels, fused_body(): pl.pallas_call(functools.partial(store_kernel, pieces), out_shape=[jax.Sh...  1.03 us

profile of v2, /device:TPU:0, one launch (start us, length us, event | category | flops | bytes accessed | tf_op | source)
XLA Modules:
  0.0 35.3 jit_solution(12597480580012826779)
XLA Ops:
  0.6 33.7 %shard_map.59 = (f32[2,32,32,128]{3,2,1,0:T(8,128)S(1)}, f32[2,32,32,128]{3,2,1,0:T(8,128)S(1)}) custom-call(f32[32,32,128]{2,1,0:T(8,128)} %f_hbm.1, f32[1,128]{1,0:T(1,128)} %bitcast.1, f32[5]{0:T(128)} %e_hbm.1, f32[5,128,128]{2,1,0:T(8,128)} %g_hbm.1), custom_call_target="tpu_custom_call" | custom-call | tf_op jit(solution)/shard_map/pallas_call | solution.py:866
  34.3 1.0 %shard_map.60 = (f32[32,32,128]{2,1,0:T(8,128)}, f32[32,32,128]{2,1,0:T(8,128)}) custom-call(f32[2,32,32,128]{3,2,1,0:T(8,128)S(1)} %get-tuple-element.4.sol_v, f32[2,32,32,128]{3,2,1,0:T(8,128)S(1)} %get-tuple-element.5.res_v), custom_call_target="tpu_custom_call" | custom-call | tf_op jit(solution)/shard_map/pallas_call | solution.py:883

commit v3 on v2

--- a/solution.py
+++ b/solution.py
@@ -184,6 +184,7 @@
 YPAD = 8
 SPARE = 32
 DEEPEST = 3
+NEAR = 2
 
 
 def block_range(offset, own, halo, extent):
@@ -195,6 +196,33 @@
 
 def round_up(value, unit):
     return -(-value // unit) * unit
+
+
+def difference(outer, inner):
+    (a, b), (c, d) = outer
+    (e, f), (g, h) = inner
+    if e >= f or g >= h:
+        return [outer]
+    parts = [((a, e), (c, d)), ((f, b), (c, d)), ((e, f), (c, g)), ((e, f), (h, d))]
+    return [(x, y) for x, y in parts if x[0] < x[1] and y[0] < y[1]]
+
+
+def needed(t, dy, own, size, halo):
+    (n0, n1), (s0, s1) = own, size
+    x = max(0, t * n0 - halo), min(s0, (t + 1) * n0 + halo)
+    y = max(0, dy * n1 - halo), min(s1, (dy + 1) * n1 + halo)
+    return x, y
+
+
+def both_parts(t, dy, own, size, halo):
+    near = needed(t, dy, own, size, NEAR)
+    inner = [near] if near[0][0] < near[0][1] and near[1][0] < near[1][1] else []
+    outer = difference(needed(t, dy, own, size, halo), near)
+    return inner, outer
+
+
+def area(parts):
+    return sum((x[1] - x[0]) * (y[1] - y[0]) for x, y in parts)
 
 
 def split_planes(count, rows):
@@ -213,6 +241,7 @@
     (U1, G1, U2, G2, c3u, c3g, c4u, c4g, cwu, cwg) = take(10)
     UP, GP = [None, U1, U2, c3u, c4u], [None, G1, G2, c3g, c4g]
     own3, pool = take(2)
+    N = take(DEEPEST)
     (in_sem, g_send, g_recv, h_send, h_recv, y_recv, p_sem) = take(7)
     y_send, x_send, x_recv, o_send, o_recv = [p_sem.at[i] for i in range(5)]
 
@@ -306,81 +335,90 @@
                 def _():
                     take_rows(sem, table[low][first])
 
-    def start_copies():
-        out = []
-        reach = -(-HALOS[0] // nx)
-        for t in range(-reach, gz_n + reach):
-            xs, xn, xd = block_range(t, nx, HALOS[0], nx * gz_n)
-            dgx, target = t // gz_n, t % gz_n
-            for dy in (-1, 0, 1):
-                ys, yn, yd = block_range(dy, ny, ROWS[0], ny)
-                yd += YPAD - ROWS[0]
-                out.append((t, dgx, target, dy, (xs, xn, xd), (ys, yn, yd)))
-        return out
-
-    plan0 = start_copies()
-    R0 = X[0][0]
+    near0, far0 = N[0], X[0][0]
+    plan0 = []
+    reach = -(-ROWS[0] // nx)
+    for t in range(-reach, gz_n + reach):
+        for dy in (-1, 0, 1):
+            parts0 = both_parts(t, dy, (nx, ny), (nx * gz_n, ny), ROWS[0])
+            plan0.append((t, t // gz_n, t % gz_n, dy, parts0))
+
+    def target0(window, part, t, dy, source_z):
+        (x0, x1), (y0, y1) = part
+        p, r = x0 - t * nx + HALOS[0], y0 - dy * ny + YPAD
+        return window.at[pl.ds(p, x1 - x0), source_z, pl.ds(r, y1 - y0), :]
+
     local0 = []
-    for entry in plan0:
-        t, dgx, target, dy, (xs, xn, xd), (ys, yn, yd) = entry
+    for t, dgx, target, dy, parts0 in plan0:
         if dgx == 0 and dy == 0:
-            move = pltpu.make_async_copy(
-                f_hbm.at[pl.ds(xs, xn)],
-                R0.at[pl.ds(xd, xn), target, pl.ds(yd, yn), :],
-                in_sem.at[5],
-            )
-            local0.append((target, move))
-
-    for target, move in local0:
+            for which, window in enumerate((near0, far0)):
+                for part in parts0[which]:
+                    (x0, x1), (y0, y1) = part
+                    move = pltpu.make_async_copy(
+                        f_hbm.at[pl.ds(x0, x1 - x0), pl.ds(y0, y1 - y0), :],
+                        target0(window, part, t, dy, target),
+                        in_sem.at[5 + which],
+                    )
+                    local0.append((target, which, move))
+
+    for target, _, move in local0:
 
         @pl.when(iz == target)
         def _():
             move.start()
 
-    def copy0(entry, source_z, device):
-        t, dgx, target, dy, (xs, xn, xd), (ys, yn, yd) = entry
-        return copy(
-            f_v.at[pl.ds(xs, xn), pl.ds(ys, yn), :],
-            R0.at[pl.ds(xd, xn), source_z, pl.ds(yd, yn), :],
-            h_send.at[0],
-            h_recv.at[0],
-            device,
-        )
-
-    def send0():
-        for entry in plan0:
-            t, dgx, target, dy = entry[:4]
+    def local_done(which):
+        for target, other, move in local0:
+            if other == which:
+
+                @pl.when(iz == target)
+                def _():
+                    move.wait()
+
+    def send0(which):
+        for t, dgx, target, dy, parts0 in plan0:
             ok = inside(ix + dgx, iy + dy)
             if dgx == 0 and dy == 0:
                 ok = ok & (iz != target)
 
             @pl.when(ok)
             def _():
-                copy0(entry, iz, (ix + dgx, iy + dy, target)).start()
+                for part in parts0[which]:
+                    (x0, x1), (y0, y1) = part
+                    copy(
+                        f_v.at[pl.ds(x0, x1 - x0), pl.ds(y0, y1 - y0), :],
+                        target0((near0, far0)[which], part, t, dy, iz),
+                        h_send.at[0],
+                        h_recv.at[0, which],
+                        (ix + dgx, iy + dy, target),
+                    ).start()
 
     def in_grid(b, y):
         return 0 <= b < bx_n and 0 <= y < gy_n
 
     def sent0(b, y):
         total = 0
-        for t, dgx, target, dy, (_, xn, _), (_, yn, _) in plan0:
+        for t, dgx, target, dy, parts0 in plan0:
             there = (b // gz_n + dgx) * gz_n + target
             if in_grid(there, y + dy) and (there, dy) != (b, 0):
-                total += xn * yn
+                total += area(parts0[0]) + area(parts0[1])
         return total
 
-    def received0(b, y):
-        total = 0
-        for t, dgx, target, dy, (_, xn, _), (_, yn, _) in plan0:
-            for source_z in range(gz_n):
-                there = (b // gz_n - dgx) * gz_n + source_z
-                if target == b % gz_n and in_grid(there, y - dy) and (there, dy) != (b, 0):
-                    total += xn * yn
-        return total
+    def received0(which):
+        def count(b, y):
+            total = 0
+            for t, dgx, target, dy, parts0 in plan0:
+                for source_z in range(gz_n):
+                    there = (b // gz_n - dgx) * gz_n + source_z
+                    ok = target == b % gz_n and in_grid(there, y - dy)
+                    if ok and (there, dy) != (b, 0):
+                        total += area(parts0[which])
+            return total
+
+        return count
 
     def clear_edges():
-        for level in range(DEEPEST):
-            window = X[level][0]
+        for level, window in [(k, w) for k in range(DEEPEST) for w in (N[k], X[k][0])]:
             planes, zb, rows, lanes = window.shape
             halo = HALOS[level]
             n0, n1 = owned(level)
@@ -455,13 +493,15 @@
         y = y + iy * n1 - YPAD
         return jnp.where((y >= 0) & (y < gy_n * n1), 1.0, 0.0).astype(f32)
 
-    def region(level, shrink):
+    def region(level, shrink=0):
         if level < DEEPEST:
-            n0, n1 = owned(level)
-            h = ROWS[level] - shrink
-            return HALOS[level] - h, n0 + 2 * h, YPAD - h, round_up(n1 + 2 * h, 8)
+            return nearby(level, ROWS[level] - shrink)
         window = X[level][0].shape
         return 1, window[0] - 2, YPAD, window[2] - 2 * YPAD
+
+    def nearby(level, h):
+        n0, n1 = owned(level)
+        return HALOS[level] - h, n0 + 2 * h, YPAD - h, round_up(n1 + 2 * h, 8)
 
     def weights(level, p, c, r0, rows):
         e = e_ref[level]
@@ -583,57 +623,61 @@
                 total = around(C[level], k, p, c, r0, rows) * w
                 target[pl.ds(p, c), k, pl.ds(r0, rows)] = at(target) + (total - at(E[level]))
 
-    def spans(own, reach, width, start):
-        out = {0: (start - 1, own + 2)}
-        near = 2
-        for t in range(1, reach + 1):
-            far = min(width, t * own + 1)
-            if far >= near:
-                out[t] = (start - far, far - near + 1)
-                out[-t] = (start + own - 1 + near, far - near + 1)
-            near = far + 1
-        return out
-
-    def exchange(level, meanwhile):
+    def exchange(level):
         n0, n1 = owned(level)
         width = ROWS[level]
-        window = X[level][0]
-        along_x = spans(n0, -(-width // n0), width, HALOS[level])
-        along_y = spans(n1, 1, width, YPAD)
-        pieces = [(t, dy) for t in along_x for dy in along_y if t or dy]
-
-        def valid(x, y):
-            return (x >= 0) & (x < bx_n) & (y >= 0) & (y < gy_n)
-
-        for t, dy in pieces:
-            (p, planes), (r, rows) = along_x[t], along_y[dy]
-            there = bx + t + bx_n
-
-            @pl.when(valid(bx + t, iy + dy))
-            def _():
-                copy(
-                    window.at[pl.ds(p + t * n0, planes), :, pl.ds(r + dy * n1, rows), :],
-                    window.at[pl.ds(p, planes), :, pl.ds(r, rows), :],
-                    h_send.at[level],
-                    h_recv.at[level],
-                    (there // gz_n - gx_n, iy + dy, lax.rem(there, gz_n)),
-                ).start()
-
-        def total(sign):
+        halo = HALOS[level]
+        reach = -(-width // n0)
+        pieces = [
+            (t, dy, both_parts(t, dy, (n0, n1), (n0, n1), width))
+            for t in range(-reach, reach + 1)
+            for dy in (-1, 0, 1)
+            if t or dy
+        ]
+
+        for which, window in enumerate((N[level], X[level][0])):
+            for t, dy, parts in pieces:
+                there = bx + t + bx_n
+                x, y = bx + t, iy + dy
+
+                @pl.when((x >= 0) & (x < bx_n) & (y >= 0) & (y < gy_n))
+                def _():
+                    for (x0, x1), (y0, y1) in parts[which]:
+                        p, r = x0 - t * n0 + halo, y0 - dy * n1 + YPAD
+                        copy(
+                            N[level].at[
+                                pl.ds(halo + x0, x1 - x0), :, pl.ds(YPAD + y0, y1 - y0), :
+                            ],
+                            window.at[pl.ds(p, x1 - x0), :, pl.ds(r, y1 - y0), :],
+                            h_send.at[level],
+                            h_recv.at[level, which],
+                            (there // gz_n - gx_n, y, lax.rem(there, gz_n)),
+                        ).start()
+
+        def total(sign, wanted):
             def count(b, y):
                 return sum(
-                    gz_n * along_x[t][1] * along_y[dy][1]
-                    for t, dy in pieces
+                    gz_n * area(parts[which])
+                    for t, dy, parts in pieces
+                    for which in wanted
                     if in_grid(b + sign * t, y + sign * dy)
                 )
 
             return count
 
-        meanwhile()
-        settle(h_recv.at[level], total(-1))
-        return lambda: settle(h_send.at[level], total(1))
-
-    def gather_all():
+        arrive = lambda which: settle(h_recv.at[level, which], total(-1, (which,)))
+        return arrive, lambda: settle(h_send.at[level], total(1, (0, 1)))
+
+    def widen(level, arrive):
+        n0, n1 = owned(level)
+        rows = pl.ds(YPAD - NEAR, n1 + 2 * NEAR)
+        for p in range(HALOS[level] - NEAR, HALOS[level] + n0 + NEAR):
+            X[level][0][p, :, rows] = N[level][p, :, rows]
+        arrive(1)
+        relax(level, X[level][0], X[level][1], region(level, 1))
+        relax(level, X[level][1], X[level][2], region(level, 2))
+
+    def gather_all(meanwhile):
         def line_y(other, slot):
             return copy(own3, gather.at[bx, slot], y_send, y_recv.at[slot], (ix, other, iz))
 
@@ -653,6 +697,7 @@
         others(iy, gy_n, lambda y: line_y(y, iy).start())
         others(bx, bx_n, lambda x: line_x(own3, x, bx, iy).start())
         gather[bx, iy] = own3[...]
+        meanwhile()
         for distance in range(1, gy_n):
             for y in (iy + distance, iy - distance):
 
@@ -681,48 +726,54 @@
 
         return drains
 
-    clear_edges()
     f_load.wait()
     pl.semaphore_wait(barrier, partners)
-    send0()
+    send0(0)
     for c in loads:
         c.wait()
     setups = [setup_copies(other) for other in range(1, gz_n)]
     for group in setups:
-        for c in group:
+        for c in group[:2]:
             c.start()
+    send0(1)
+    for group in setups:
+        group[2].start()
+    clear_edges()
     for group in setups:
         for c in group[:2]:
             c.wait()
     assemble(0, 0)
-    for target, move in local0:
-
-        @pl.when(iz == target)
-        def _():
-            move.wait()
-
-    settle(h_recv.at[0], received0)
-    drains = [lambda: settle(h_send.at[0], sent0)]
+    local_done(0)
+
+    def arrive0(which):
+        if which:
+            local_done(1)
+        settle(h_recv.at[0, which], received0(which))
 
     def later():
         for group in setups:
             group[2].wait()
         lax.fori_loop(1, levels, assemble, 0)
 
+    arrive = arrive0
+    drains = [lambda: settle(h_send.at[0], sent0)]
     for level in range(DEEPEST):
+        arrive(0)
         one, two = X[level][1], X[level][2]
-        relax(level, X[level][0], one, region(level, 1))
-        relax(level, one, two, region(level, 2))
+        relax(level, N[level], one, nearby(level, 1))
+        relax(level, one, two, nearby(level, 0))
         n0, n1 = owned(level + 1)
         p, r = HALOS[level], YPAD
         if level < DEEPEST - 1:
-            to_plane = HALOS[level + 1] - 1
-            window = X[level + 1][0]
-            restrict_planes(level, window, n0 + 2, p - 2, r - 2, to_plane, YPAD - 1, n1 + 2)
-            drains.append(exchange(level + 1, (later, clear_coarse)[level]))
+            restrict_planes(level, N[level + 1], n0, p, r, HALOS[level + 1], YPAD, n1)
+            following, drain = exchange(level + 1)
+            drains.append(drain)
+            (later, clear_coarse)[level]()
+            widen(level, arrive)
+            arrive = following
         else:
             restrict_planes(level, own3, n0, p, r, 0, 0, n1)
-            drains.append(gather_all())
+            drains.append(gather_all(lambda: widen(level, arrive)))
 
     whole3, whole4 = region(3, 0), region(4, 0)
     relax(3, X[3][0], X[3][1], whole3)
@@ -763,16 +814,11 @@
             block = ref.at[there, pl.ds(iz * nx + p, c)]
             copy(block, block, o_send, o_recv, (ix, iy, there)).start()
 
-    quarter = nx // 4
-    own0 = [(HALOS[0] + p, quarter, YPAD, ny) for p in range(0, nx, quarter)]
-    for where in own0:
-        p = where[0] - HALOS[0]
-        collect(0, where, place=iz * nx + p)
-        send_out(sol_ref, p, quarter)
-    for where in own0:
-        p = where[0] - HALOS[0]
-        relax(0, X[0][3], res_ref, where, place=iz * nx + p)
-        send_out(res_ref, p, quarter)
+    own0 = nearby(0, 0)
+    collect(0, own0, place=iz * nx)
+    send_out(sol_ref, 0, nx)
+    relax(0, X[0][3], res_ref, own0, place=iz * nx)
+    send_out(res_ref, 0, nx)
     for drain in drains:
         drain()
     for sem in (o_send, o_recv):
@@ -854,9 +900,10 @@
         + [vmem(windows[2])] * 2
         + [vmem(c3), vmem(c3), vmem(c4), vmem(c4), vmem(cw), vmem(cw)]
         + [vmem(own(3)), vmem((most, depth))]
-        + [dma((6,))]
+        + [vmem(w) for w in windows[:DEEPEST]]
+        + [dma((7,))]
         + [dma((gz_n, 3))] * 2
-        + [dma((DEEPEST,))] * 2
+        + [dma((DEEPEST,)), dma((DEEPEST, 2))]
         + [dma((gy_n,)), dma((5,))]
     )
     in_vmem = pl.BlockSpec(memory_space=pltpu.VMEM)

time: 35.5 us -> 32 us (0.901)
  Pallas kernels: 34.7 us -> 31.2 us
    pallas_call x1, Pallas kernels: 33.7 us -> 30.2 us  [fused_body(): pl.pallas_call(functools.partial(cycle_kernel, (gx_n, gy_n, gz_n, nx, ny,...]
where the time goes in v3:
time: 32 us; the launch traced here: 31.8 us
  Pallas kernels  31.2 us (98%)
  between operations  0.64 us (2%)
    pallas_call x1, Pallas kernels, fused_body(): pl.pallas_call(functools.partial(cycle_kernel, (gx_n, gy_n, gz_n, nx, ny,...  30.2 us
    pallas_call x1, Pallas kernels, fused_body(): pl.pallas_call(functools.partial(store_kernel, pieces), out_shape=[jax.Sh...  1.03 us

profile of v3, /device:TPU:0, one launch (start us, length us, event | category | flops | bytes accessed | tf_op | source)
XLA Modules:
  0.0 31.8 jit_solution(4825052126392104380)
XLA Ops:
  0.6 30.2 %shard_map.59 = (f32[2,32,32,128]{3,2,1,0:T(8,128)S(1)}, f32[2,32,32,128]{3,2,1,0:T(8,128)S(1)}) custom-call(f32[32,32,128]{2,1,0:T(8,128)} %f_hbm.1, f32[1,128]{1,0:T(1,128)} %bitcast.1, f32[5]{0:T(128)} %e_hbm.1, f32[5,128,128]{2,1,0:T(8,128)} %g_hbm.1), custom_call_target="tpu_custom_call" | custom-call | tf_op jit(solution)/shard_map/pallas_call | solution.py:913
  30.8 1.0 %shard_map.60 = (f32[32,32,128]{2,1,0:T(8,128)}, f32[32,32,128]{2,1,0:T(8,128)}) custom-call(f32[2,32,32,128]{3,2,1,0:T(8,128)S(1)} %get-tuple-element.4.sol_v, f32[2,32,32,128]{3,2,1,0:T(8,128)S(1)} %get-tuple-element.5.res_v), custom_call_target="tpu_custom_call" | custom-call | tf_op jit(solution)/shard_map/pallas_call | solution.py:930

commit v4 on v3

--- a/solution.py
+++ b/solution.py
@@ -207,18 +207,23 @@
     return [(x, y) for x, y in parts if x[0] < x[1] and y[0] < y[1]]
 
 
-def needed(t, dy, own, size, halo):
-    (n0, n1), (s0, s1) = own, size
-    x = max(0, t * n0 - halo), min(s0, (t + 1) * n0 + halo)
-    y = max(0, dy * n1 - halo), min(s1, (dy + 1) * n1 + halo)
+def needed(t, dy, own, size, halos):
+    (n0, n1), (s0, s1), (left, right, side) = own, size, halos
+    x = max(0, t * n0 - left), min(s0, (t + 1) * n0 + right)
+    y = max(0, dy * n1 - side), min(s1, (dy + 1) * n1 + side)
     return x, y
 
 
-def both_parts(t, dy, own, size, halo):
-    near = needed(t, dy, own, size, NEAR)
-    inner = [near] if near[0][0] < near[0][1] and near[1][0] < near[1][1] else []
-    outer = difference(needed(t, dy, own, size, halo), near)
-    return inner, outer
+def vacant(part):
+    return any(low >= high for low, high in part)
+
+
+def both_parts(t, dy, own, size, near, far):
+    whole = needed(t, dy, own, size, far)
+    inner = needed(t, dy, own, size, near) if near else ((0, 0), (0, 0))
+    common = tuple((max(a, c), min(b, d)) for (a, b), (c, d) in zip(whole, inner))
+    outer = [] if vacant(whole) else difference(whole, common)
+    return [] if vacant(inner) else [inner], outer
 
 
 def area(parts):
@@ -234,21 +239,26 @@
     refs = iter(scratch)
     take = lambda count: [next(refs) for _ in range(count)]
     sinv, g_all, z_all, gather, f_v, e_ref = take(6)
-    X = [take(4) for _ in range(DEEPEST + 1)]
-    X.append(take(2))
+    X = [take(3) for _ in range(DEEPEST + 1)]
+    X.append(take(1))
     C = take(DEEPEST + 1)
     E = take(DEEPEST + 1)
     (U1, G1, U2, G2, c3u, c3g, c4u, c4g, cwu, cwg) = take(10)
     UP, GP = [None, U1, U2, c3u, c4u], [None, G1, G2, c3g, c4g]
     own3, pool = take(2)
+    T = take(DEEPEST + 1)
     N = take(DEEPEST)
     (in_sem, g_send, g_recv, h_send, h_recv, y_recv, p_sem) = take(7)
+    r_send, r_recv = take(2)
     y_send, x_send, x_recv, o_send, o_recv = [p_sem.at[i] for i in range(5)]
 
     ix, iy, iz = lax.axis_index("gx"), lax.axis_index("gy"), lax.axis_index("gz")
     bx = ix * gz_n + iz
     bx_n = gx_n * gz_n
     f32 = jnp.float32
+
+    whole = gz_n * depth
+    keep = 1.0 - damping
 
     def owned(level):
         return nx >> level, ny >> level
@@ -290,7 +300,7 @@
     for dx in range(1 - bx_n, bx_n):
         for dy in range(1 - gy_n, gy_n):
             close = abs(dx) <= reach_all and abs(dy) <= 1
-            if (dx == 0 and dy == 0) or not (close or dx == 0 or dy == 0):
+            if (dx == 0 and dy == 0) or not close:
                 continue
             x, y = bx + dx, iy + dy
             ok = (x >= 0) & (x < bx_n) & (y >= 0) & (y < gy_n)
@@ -340,8 +350,10 @@
     reach = -(-ROWS[0] // nx)
     for t in range(-reach, gz_n + reach):
         for dy in (-1, 0, 1):
-            parts0 = both_parts(t, dy, (nx, ny), (nx * gz_n, ny), ROWS[0])
+            near_halo, far_halo = (NEAR,) * 3, (ROWS[0],) * 3
+            parts0 = both_parts(t, dy, (nx, ny), (nx * gz_n, ny), near_halo, far_halo)
             plan0.append((t, t // gz_n, t % gz_n, dy, parts0))
+    plan0.sort(key=lambda entry: -abs(entry[1]) - abs(entry[3]))
 
     def target0(window, part, t, dy, source_z):
         (x0, x1), (y0, y1) = part
@@ -450,18 +462,26 @@
                     0, planes, lambda i, c: zero_rows(window, i, YPAD + n1, edge), 0
                 )
 
-    def fill(ref):
-        zero = jnp.zeros(ref.shape[1:], f32)
+    def fill_border(ref, side):
+        planes, zb, rows, lanes = ref.shape
+        plane = jnp.zeros((side, zb, rows, lanes), f32)
+        edge = jnp.zeros((zb, YPAD, lanes), f32)
+        ref[0:side] = plane
+        ref[planes - side : planes] = plane
 
         def step(i, _):
-            ref[i] = zero
+            ref[i, :, pl.ds(0, YPAD)] = edge
+            ref[i, :, pl.ds(rows - YPAD, YPAD)] = edge
             return 0
 
-        lax.fori_loop(0, ref.shape[0], step, 0)
+        lax.fori_loop(side, planes - side, step, 0, unroll=4)
 
     def clear_coarse():
-        for ref in (*X[3][:3], C[3], X[4][0], c3u, c3g, c4u, c4g):
-            fill(ref)
+        side = HALOS[2] // 2 + 1
+        for ref in (X[3][0], X[3][2], T[3], C[3], X[4][0], c4u, c4g):
+            fill_border(ref, 1)
+        for ref in (c3u, c3g):
+            fill_border(ref, side)
 
     def assemble(level, _):
         merged = g_all[level, 0]
@@ -479,7 +499,10 @@
             top = top + merged[:, size - 1 : size] * p_row
             low = low + block[:, 0:1] * q_row
             merged = jnp.concatenate([top, low], 0)
-        sinv[level] = (damping * merged).astype(jnp.bfloat16)
+        solve = (damping * merged).astype(jnp.bfloat16)
+        sinv[level, pl.ds(0, whole), :] = solve
+        twice = jnp.dot(solve, solve, preferred_element_type=f32)
+        sinv[level, pl.ds(whole, whole), :] = twice.astype(jnp.bfloat16)
         return 0
 
     def plane_mask(level, i):
@@ -499,9 +522,10 @@
         window = X[level][0].shape
         return 1, window[0] - 2, YPAD, window[2] - 2 * YPAD
 
-    def nearby(level, h):
+    def nearby(level, h, extra=0):
         n0, n1 = owned(level)
-        return HALOS[level] - h, n0 + 2 * h, YPAD - h, round_up(n1 + 2 * h, 8)
+        first = HALOS[level] - h - extra
+        return first, n0 + 2 * h + extra, YPAD - h, round_up(n1 + 2 * h, 8)
 
     def weights(level, p, c, r0, rows):
         e = e_ref[level]
@@ -519,45 +543,89 @@
         at = lambda dp, dr: src[pl.ds(p + dp, c), k, pl.ds(r0 + dr, rows)]
         return (at(-1, 0) + at(1, 0)) + (at(0, -1) + at(0, 1))
 
-    def line_solve(level, fields):
-        flat = [v.reshape(-1, depth) for v in fields]
+    def product(level, first, *groups):
+        flat = [v.reshape(-1, depth) for fields in groups for v in fields]
         lhs = jnp.concatenate(flat, 1).astype(jnp.bfloat16)
-        out = jnp.dot(lhs, sinv[level], preferred_element_type=f32)
-        shape = fields[0].shape
-        return [out[:, k * depth : (k + 1) * depth].reshape(shape) for k in range(len(flat))]
-
-    def relax(level, src, dst, where, place=None):
+        rhs = sinv[level, pl.ds(first * whole, len(groups) * whole), :]
+        out = jnp.dot(lhs, rhs, preferred_element_type=f32)
+        shape = groups[0][0].shape
+        return [out[:, k * depth : (k + 1) * depth].reshape(shape) for k in range(gz_n)]
+
+    def relax(level, src, dst, where):
         for p, c, r0, rows in chunks(where):
             w = weights(level, p, c, r0, rows)
             total = [around(src, k, p, c, r0, rows) * w for k in range(gz_n)]
-            out = line_solve(level, total)
+            out = product(level, 0, total)
             for k in range(gz_n):
-                value = (1.0 - damping) * src[pl.ds(p, c), k, pl.ds(r0, rows)] + out[k]
-                if place is None:
-                    dst[pl.ds(p, c), k, pl.ds(r0, rows)] = value
-                else:
-                    dst[k, pl.ds(place + p - where[0], c)] = value
-
-    def collect(level, where, place=None, offset=0):
+                value = keep * src[pl.ds(p, c), k, pl.ds(r0, rows)] + out[k]
+                dst[pl.ds(p, c), k, pl.ds(r0, rows)] = value
+
+    def spread(level, src, where):
+        for p, c, r0, rows in chunks(where):
+            w = weights(level, p, c, r0, rows)
+            for k in range(gz_n):
+                T[level][pl.ds(p, c), k, pl.ds(r0, rows)] = around(src, k, p, c, r0, rows) * w
+
+    def relax_twice(level, src, where, once, put):
+        for p, c, r0, rows in chunks(where):
+            w = weights(level, p, c, r0, rows)
+            at = lambda ref, k: ref[pl.ds(p, c), k, pl.ds(r0, rows)]
+            one = [at(T[level], k) for k in range(gz_n)]
+            two = [around(T[level], k, p, c, r0, rows) * w for k in range(gz_n)]
+            if once is None:
+                out = product(level, 0, [2.0 * keep * v for v in one], two)
+            else:
+                first, second = product(level, 0, one), product(level, 1, two)
+                out = [second[k] + 2.0 * keep * first[k] for k in range(gz_n)]
+            for k in range(gz_n):
+                value = at(src, k)
+                if once is not None:
+                    once[pl.ds(p, c), k, pl.ds(r0, rows)] = keep * value + first[k]
+                put(k, p, c, r0, rows, keep * keep * value + out[k])
+
+    def into(ref):
+        def put(k, p, c, r0, rows, value):
+            ref[pl.ds(p, c), k, pl.ds(r0, rows)] = value
+
+        return put
+
+    def sums(level, p, c, r0, rows):
+        at = lambda ref, k: ref[pl.ds(p, c), k, pl.ds(r0, rows)]
+        last = X[level][-1]
+        total = []
+        for k in range(gz_n):
+            value = (1.0 + keep) * at(last, k)
+            if level <= DEEPEST:
+                value = value + (at(X[level][0], k) + at(X[level][1], k))
+            total.append(value)
+        return total
+
+    def finish(level, where, offset=0):
+        last = X[level][-1]
+        for p, c, r0, rows in chunks(where):
+            w = weights(level, p, c, r0, rows)
+            at = lambda ref, k: ref[pl.ds(p, c), k, pl.ds(r0, rows)]
+            total = sums(level, p, c, r0, rows)
+            side = [around(last, k, p, c, r0, rows) * w for k in range(gz_n)]
+            rest = product(level, 0, side)
+            u = product(level, 0, total, side)
+            for k in range(gz_n):
+                if level <= DEEPEST:
+                    u[k] = u[k] + at(C[level], k)
+                g = damping * (total[k] + rest[k])
+                g = g + (4.0 * (e_ref[level - 1] - e_ref[level])) * u[k]
+                if level <= DEEPEST:
+                    g = g + at(E[level], k)
+                UP[level][pl.ds(p + offset, c), k, pl.ds(r0, rows)] = u[k]
+                GP[level][pl.ds(p + offset, c), k, pl.ds(r0, rows)] = g
+
+    def finest(where, place):
         for p, c, r0, rows in chunks(where):
             at = lambda ref, k: ref[pl.ds(p, c), k, pl.ds(r0, rows)]
-            total = []
+            total = sums(0, p, c, r0, rows)
+            u = product(0, 0, total, [at(T[0], k) for k in range(gz_n)])
             for k in range(gz_n):
-                part = [at(ref, k) for ref in X[level]]
-                while len(part) > 1:
-                    part = [part[i] + part[i + 1] for i in range(0, len(part), 2)]
-                total.append(part[0])
-            out = line_solve(level, total)
-            for k in range(gz_n):
-                u = out[k] if level > DEEPEST else out[k] + at(C[level], k)
-                if level == 0:
-                    sol_ref[k, pl.ds(place + p - where[0], c)] = u
-                    continue
-                g = damping * total[k] + (4.0 * (e_ref[level - 1] - e_ref[level])) * u
-                if level <= DEEPEST:
-                    g = g + at(E[level], k)
-                UP[level][pl.ds(p + offset, c), k, pl.ds(r0, rows)] = u
-                GP[level][pl.ds(p + offset, c), k, pl.ds(r0, rows)] = g
+                sol_ref[k, pl.ds(place + p - where[0], c)] = u[k] + at(C[0], k)
 
     def restrict_planes(level, dst, planes, x0, y0, to_plane, to_row, rows):
         src = X[level][2]
@@ -623,106 +691,187 @@
                 total = around(C[level], k, p, c, r0, rows) * w
                 target[pl.ds(p, c), k, pl.ds(r0, rows)] = at(target) + (total - at(E[level]))
 
+    def near_halos(level, core):
+        if level < DEEPEST - 1:
+            return (NEAR,) * 3
+        if core < gz_n - 1:
+            return None
+        return NEAR + owned(level)[0] * core, NEAR, NEAR
+
+    def far_halos(level, core):
+        width = ROWS[level]
+        return (0 if core else width), (width if core else 0), width
+
+    def relay(level):
+        n0, n1 = owned(level)
+        width, halo = ROWS[level], HALOS[level]
+        rows = pl.ds(YPAD - width, n1 + 2 * width)
+        window = X[level][0]
+        def move(core):
+            src, dst = ((halo + n0 - width, halo - width), (halo, halo + n0))[core]
+            return copy(
+                window.at[pl.ds(src, width), :, rows, :],
+                window.at[pl.ds(dst, width), :, rows, :],
+                r_send.at[level - 1],
+                r_recv.at[level - 1],
+                (ix, iy, 1 - core),
+            )
+
+        return move
+
     def exchange(level):
         n0, n1 = owned(level)
         width = ROWS[level]
         halo = HALOS[level]
         reach = -(-width // n0)
-        pieces = [
-            (t, dy, both_parts(t, dy, (n0, n1), (n0, n1), width))
-            for t in range(-reach, reach + 1)
-            for dy in (-1, 0, 1)
-            if t or dy
-        ]
-
-        for which, window in enumerate((N[level], X[level][0])):
+        pieces = []
+        for t in range(-reach, reach + 1):
+            for dy in (-1, 0, 1):
+                if t or dy:
+                    parts = [
+                        both_parts(
+                            t,
+                            dy,
+                            (n0, n1),
+                            (n0, n1),
+                            near_halos(level, core),
+                            far_halos(level, core),
+                        )
+                        for core in range(gz_n)
+                    ]
+                    pieces.append((t, dy, parts))
+        pieces.sort(key=lambda piece: -abs(piece[0]) - abs(piece[1]))
+
+        def start(which):
+            window = (N[level], X[level][0])[which]
             for t, dy, parts in pieces:
                 there = bx + t + bx_n
+                core = lax.rem(there, gz_n)
                 x, y = bx + t, iy + dy
-
-                @pl.when((x >= 0) & (x < bx_n) & (y >= 0) & (y < gy_n))
-                def _():
-                    for (x0, x1), (y0, y1) in parts[which]:
-                        p, r = x0 - t * n0 + halo, y0 - dy * n1 + YPAD
-                        copy(
-                            N[level].at[
-                                pl.ds(halo + x0, x1 - x0), :, pl.ds(YPAD + y0, y1 - y0), :
-                            ],
-                            window.at[pl.ds(p, x1 - x0), :, pl.ds(r, y1 - y0), :],
-                            h_send.at[level],
-                            h_recv.at[level, which],
-                            (there // gz_n - gx_n, y, lax.rem(there, gz_n)),
-                        ).start()
+                alike = all(part == parts[0] for part in parts)
+                for target in range(1 if alike else gz_n):
+                    ok = (x >= 0) & (x < bx_n) & (y >= 0) & (y < gy_n)
+                    if not alike:
+                        ok = ok & (core == target)
+                    if not parts[target][which]:
+                        continue
+
+                    @pl.when(ok)
+                    def _():
+                        for (x0, x1), (y0, y1) in parts[target][which]:
+                            p, r = x0 - t * n0 + halo, y0 - dy * n1 + YPAD
+                            copy(
+                                N[level].at[
+                                    pl.ds(halo + x0, x1 - x0),
+                                    :,
+                                    pl.ds(YPAD + y0, y1 - y0),
+                                    :,
+                                ],
+                                window.at[pl.ds(p, x1 - x0), :, pl.ds(r, y1 - y0), :],
+                                h_send.at[level],
+                                h_recv.at[level, which],
+                                (there // gz_n - gx_n, y, core),
+                            ).start()
 
         def total(sign, wanted):
             def count(b, y):
-                return sum(
-                    gz_n * area(parts[which])
-                    for t, dy, parts in pieces
-                    for which in wanted
-                    if in_grid(b + sign * t, y + sign * dy)
-                )
+                rows = 0
+                for t, dy, parts in pieces:
+                    if in_grid(b + sign * t, y + sign * dy):
+                        core = (b + t) % gz_n if sign > 0 else b % gz_n
+                        rows += sum(gz_n * area(parts[core][which]) for which in wanted)
+                return rows
 
             return count
 
         arrive = lambda which: settle(h_recv.at[level, which], total(-1, (which,)))
-        return arrive, lambda: settle(h_send.at[level], total(1, (0, 1)))
+        return start, arrive, lambda: settle(h_send.at[level], total(1, (0, 1)))
 
     def widen(level, arrive):
         n0, n1 = owned(level)
-        rows = pl.ds(YPAD - NEAR, n1 + 2 * NEAR)
-        for p in range(HALOS[level] - NEAR, HALOS[level] + n0 + NEAR):
-            X[level][0][p, :, rows] = N[level][p, :, rows]
+        for core in range(gz_n):
+            near = near_halos(level, core) or (0, 0, 0)
+            far = far_halos(level, core) if level else near
+            left, right, side = (min(a, b) for a, b in zip(near, far))
+            rows = pl.ds(YPAD - side, n1 + 2 * side)
+
+            @pl.when(iz == core)
+            def _():
+                for p in range(HALOS[level] - left, HALOS[level] + n0 + right):
+                    X[level][0][p, :, rows] = N[level][p, :, rows]
+
         arrive(1)
+        if level:
+            for core in range(gz_n):
+
+                @pl.when(iz == core)
+                def _():
+                    relay(level)(core).start()
+
+            relay(level)(0).wait_recv()
         relax(level, X[level][0], X[level][1], region(level, 1))
         relax(level, X[level][1], X[level][2], region(level, 2))
+        if level:
+            relay(level)(0).wait_send()
 
     def gather_all(meanwhile):
+        leader = gz_n - 1
+        leading = iz == leader
+
         def line_y(other, slot):
-            return copy(own3, gather.at[bx, slot], y_send, y_recv.at[slot], (ix, other, iz))
-
-        def line_x(src, other, slot_x, slot_y):
-            return copy(
-                src,
-                gather.at[slot_x, slot_y],
-                x_send,
-                x_recv,
-                (other // gz_n, iy, lax.rem(other, gz_n)),
-            )
-
-        def others(me, count, act):
-            for s in range(1, count):
-                act(lax.rem(me + s, count))
-
-        others(iy, gy_n, lambda y: line_y(y, iy).start())
-        others(bx, bx_n, lambda x: line_x(own3, x, bx, iy).start())
-        gather[bx, iy] = own3[...]
+            return copy(own3, gather.at[ix, slot], y_send, y_recv.at[slot], (ix, other, leader))
+
+        def share(src, slot):
+            for core in range(gz_n):
+                for s in range(1, gx_n):
+                    other = (lax.rem(ix + s, gx_n), iy, core)
+                    copy(src, gather.at[ix, slot], x_send, x_recv, other).start()
+            for core in range(leader):
+                copy(src, gather.at[ix, slot], x_send, x_recv, (ix, iy, core)).start()
+
+        @pl.when(leading)
+        def _():
+            for s in range(1, gy_n):
+                line_y(lax.rem(iy + s, gy_n), iy).start()
+            share(own3, iy)
+            gather[ix, iy] = own3[...]
+            for distance in range(1, gy_n):
+                for y in (iy + distance, iy - distance):
+
+                    @pl.when((y >= 0) & (y < gy_n))
+                    def _():
+                        line_y(y, y).wait_recv()
+                        share(gather.at[ix, y], y)
+
         meanwhile()
-        for distance in range(1, gy_n):
-            for y in (iy + distance, iy - distance):
-
-                @pl.when((y >= 0) & (y < gy_n))
-                def _():
-                    line_y(y, y).wait_recv()
-                    block = gather.at[bx, y]
-                    others(bx, bx_n, lambda x: line_x(block, x, bx, y).start())
-
         size = own3.shape[0] * own3.shape[1] * own3.shape[2]
-        take_rows(x_recv, (bx_n - 1) * gy_n * size)
+
+        @pl.when(leading)
+        def _():
+            take_rows(x_recv, (gx_n - 1) * gy_n * size)
+
+        @pl.when(iz < leader)
+        def _():
+            take_rows(x_recv, gx_n * gy_n * size)
+
         n0, n1 = owned(3)
         window = X[3][0]
 
         def place(b, _):
-            for i in range(n0):
+            for i in range(gz_n * n0):
                 for y in range(gy_n):
-                    window[1 + b * n0 + i, :, pl.ds(YPAD + y * n1, n1), :] = gather[b, y, i]
+                    at = 1 + b * gz_n * n0 + i
+                    window[at, :, pl.ds(YPAD + y * n1, n1), :] = gather[b, y, i]
             return 0
 
-        lax.fori_loop(0, bx_n, place, 0)
+        lax.fori_loop(0, gx_n, place, 0)
 
         def drains():
-            take_rows(y_send, (gy_n - 1) * size)
-            take_rows(x_send, (bx_n - 1) * gy_n * size)
+            @pl.when(leading)
+            def _():
+                take_rows(y_send, (gy_n - 1) * size)
+                for _ in range(gy_n):
+                    take_rows(x_send, (gx_n * gz_n - 1) * size)
 
         return drains
 
@@ -735,10 +884,8 @@
     for group in setups:
         for c in group[:2]:
             c.start()
+    clear_edges()
     send0(1)
-    for group in setups:
-        group[2].start()
-    clear_edges()
     for group in setups:
         for c in group[:2]:
             c.wait()
@@ -759,32 +906,38 @@
     drains = [lambda: settle(h_send.at[0], sent0)]
     for level in range(DEEPEST):
         arrive(0)
-        one, two = X[level][1], X[level][2]
-        relax(level, N[level], one, nearby(level, 1))
-        relax(level, one, two, nearby(level, 0))
+        extra = owned(level)[0] * (gz_n - 1) if level == DEEPEST - 1 else 0
+        spread(level, N[level], nearby(level, 1, extra))
+        relax_twice(level, N[level], nearby(level, 0, extra), None, into(X[level][2]))
         n0, n1 = owned(level + 1)
         p, r = HALOS[level], YPAD
         if level < DEEPEST - 1:
             restrict_planes(level, N[level + 1], n0, p, r, HALOS[level + 1], YPAD, n1)
-            following, drain = exchange(level + 1)
+            start, following, drain = exchange(level + 1)
             drains.append(drain)
-            (later, clear_coarse)[level]()
-            widen(level, arrive)
+            start(0)
+            start(1)
+            if level == 0:
+                for group in setups:
+                    group[2].start()
+                widen(level, arrive)
+                later()
+            else:
+                clear_coarse()
+                widen(level, arrive)
             arrive = following
         else:
-            restrict_planes(level, own3, n0, p, r, 0, 0, n1)
+            restrict_planes(level, own3, gz_n * n0, p - extra, r, 0, 0, n1)
             drains.append(gather_all(lambda: widen(level, arrive)))
 
     whole3, whole4 = region(3, 0), region(4, 0)
-    relax(3, X[3][0], X[3][1], whole3)
-    relax(3, X[3][1], X[3][2], whole3)
+    spread(3, X[3][0], whole3)
+    relax_twice(3, X[3][0], whole3, X[3][1], into(X[3][2]))
     restrict_planes(3, X[4][0], whole4[1], 1, YPAD, 1, YPAD, whole4[3])
-    relax(4, X[4][0], X[4][1], whole4)
-    collect(4, whole4)
+    finish(4, whole4)
     correct(3, c4u, c4g, 1, YPAD)
-    relax(3, X[3][2], X[3][3], whole3)
     pad3 = HALOS[2] // 2 + 1
-    collect(3, whole3, offset=pad3 - 1)
+    finish(3, whole3, offset=pad3 - 1)
     n0, n1 = owned(3)
     margin = YPAD // 2
     for y in range(gy_n):
@@ -803,10 +956,10 @@
         else:
             x0 = HALOS[level + 1] - HALOS[level] // 2
             correct(level, UP[level + 1], GP[level + 1], x0, YPAD // 2)
-        where = region(level, 3)
-        relax(level, X[level][2], X[level][3], where)
         if level:
-            collect(level, where)
+            finish(level, region(level, 3))
+        else:
+            spread(0, X[0][2], region(0, 3))
 
     def send_out(ref, p, c):
         for other in range(1, gz_n):
@@ -815,9 +968,13 @@
             copy(block, block, o_send, o_recv, (ix, iy, there)).start()
 
     own0 = nearby(0, 0)
-    collect(0, own0, place=iz * nx)
+    finest(own0, iz * nx)
     send_out(sol_ref, 0, nx)
-    relax(0, X[0][3], res_ref, own0, place=iz * nx)
+
+    def store(k, p, c, r0, rows, value):
+        res_ref[k, pl.ds(iz * nx + p - own0[0], c)] = value
+
+    relax_twice(0, X[0][2], own0, None, store)
     send_out(res_ref, 0, nx)
     for drain in drains:
         drain()
@@ -856,7 +1013,7 @@
         and nx % 8 == 0
         and ny % 32 == 0
         and (shape[1] >> 4) % 8 == 0
-        and gz_n <= 2
+        and gz_n == 2 and gy_n <= 4
     )
 
 
@@ -881,30 +1038,31 @@
     c3 = (full3[0] - 2 + 2 * pad3,) + full3[1:]
     cw = (windows[2][0] // 2 + 2, gz_n, (ny >> 3) + 28, depth)
     most = gz_n * (nx + 2 * HALOS[0] + 8) * (ny + 2 * YPAD)
-    bx_n = gx_n * gz_n
     dma = pltpu.SemaphoreType.DMA
-    own = lambda k: (nx >> k, gz_n, ny >> k, depth)
+    chip3 = (gz_n * (nx >> 3), gz_n, ny >> 3, depth)
     scratch = (
         [
-            pltpu.VMEM((levels, gz_n * depth, gz_n * depth), jnp.bfloat16),
+            pltpu.VMEM((levels, 2 * gz_n * depth, gz_n * depth), jnp.bfloat16),
             vmem((levels, gz_n, depth, depth)),
             vmem((gz_n, 1, depth)),
-            vmem((bx_n, gy_n) + own(3)),
+            vmem((gx_n, gy_n) + chip3),
             vmem(right_side.shape),
             pltpu.SMEM((levels,), jnp.float32),
         ]
-        + [vmem(w) for w in windows[: DEEPEST + 1] for _ in range(4)]
-        + [vmem(full4)] * 2
+        + [vmem(w) for w in windows[: DEEPEST + 1] for _ in range(3)]
+        + [vmem(full4)]
         + [vmem(w) for w in windows[: DEEPEST + 1]] * 2
         + [vmem(windows[1])] * 2
         + [vmem(windows[2])] * 2
         + [vmem(c3), vmem(c3), vmem(c4), vmem(c4), vmem(cw), vmem(cw)]
-        + [vmem(own(3)), vmem((most, depth))]
+        + [vmem(chip3), vmem((most, depth))]
+        + [vmem(w) for w in windows[: DEEPEST + 1]]
         + [vmem(w) for w in windows[:DEEPEST]]
         + [dma((7,))]
         + [dma((gz_n, 3))] * 2
         + [dma((DEEPEST,)), dma((DEEPEST, 2))]
         + [dma((gy_n,)), dma((5,))]
+        + [dma((DEEPEST - 1,))] * 2
     )
     in_vmem = pl.BlockSpec(memory_space=pltpu.VMEM)
     in_hbm = pl.BlockSpec(memory_space=pltpu.HBM)

time: 32 us -> 31.7 us (level)
  no operation moved by 1% of the time
where the time goes in v4:
time: 31.7 us; the launch traced here: 31.6 us
  Pallas kernels  31 us (98%)
  between operations  0.64 us (2%)
    pallas_call x1, Pallas kernels, fused_body(): pl.pallas_call(functools.partial(cycle_kernel, (gx_n, gy_n, gz_n, nx, ny,...  29.9 us
    pallas_call x1, Pallas kernels, fused_body(): pl.pallas_call(functools.partial(store_kernel, pieces), out_shape=[jax.Sh...  1.03 us

profile of v4, /device:TPU:0, one launch (start us, length us, event | category | flops | bytes accessed | tf_op | source)
XLA Modules:
  0.0 31.6 jit_solution(3436828292197987456)
XLA Ops:
  0.6 29.9 %shard_map.59 = (f32[2,32,32,128]{3,2,1,0:T(8,128)S(1)}, f32[2,32,32,128]{3,2,1,0:T(8,128)S(1)}) custom-call(f32[32,32,128]{2,1,0:T(8,128)} %f_hbm.1, f32[1,128]{1,0:T(1,128)} %bitcast.1, f32[5]{0:T(128)} %e_hbm.1, f32[5,128,128]{2,1,0:T(8,128)} %g_hbm.1), custom_call_target="tpu_custom_call" | custom-call | tf_op jit(solution)/shard_map/pallas_call | solution.py:1071
  30.6 1.0 %shard_map.60 = (f32[32,32,128]{2,1,0:T(8,128)}, f32[32,32,128]{2,1,0:T(8,128)}) custom-call(f32[2,32,32,128]{3,2,1,0:T(8,128)S(1)} %get-tuple-element.4.sol_v, f32[2,32,32,128]{3,2,1,0:T(8,128)S(1)} %get-tuple-element.5.res_v), custom_call_target="tpu_custom_call" | custom-call | tf_op jit(solution)/shard_map/pallas_call | solution.py:1088

commit v5 on v4

--- a/solution.py
+++ b/solution.py
@@ -276,7 +276,7 @@
     def inside(x, y):
         return (x >= 0) & (x < gx_n) & (y >= 0) & (y < gy_n)
 
-    parts = 4
+    parts = 8
     span = f_v.shape[0] // parts
     for i in range(parts):
         at = pl.ds(i * span, span)
@@ -289,9 +289,6 @@
         pltpu.make_async_copy(g_hbm.at[rest], g_all.at[rest, iz], in_sem.at[3]),
         pltpu.make_async_copy(e_hbm, e_ref, in_sem.at[4]),
     ]
-    for c in loads:
-        c.start()
-
     reach_all = max(
         gz_n - 1 - (-HALOS[0] // nx), *[-(-HALOS[k] // owned(k)[0]) for k in (1, 2)]
     )
@@ -510,6 +507,11 @@
         x = bx * n0 - HALOS[level] + i
         return jnp.where((x >= 0) & (x < bx_n * n0), 1.0, 0.0).astype(f32)
 
+    def masked(level, p, value):
+        if 0 <= p - HALOS[level] < owned(level)[0]:
+            return value
+        return value * plane_mask(level, p)
+
     def row_mask(level, first, rows, stride):
         n1 = owned(level)[1]
         y = lax.broadcasted_iota(jnp.int32, (rows, depth), 0) * stride + first
@@ -531,8 +533,8 @@
         e = e_ref[level]
         if level >= DEEPEST:
             return e
-        mask = row_mask(level, r0, rows, 1)
-        return jnp.stack([mask * (e * plane_mask(level, p + i)) for i in range(c)])
+        mask = row_mask(level, r0, rows, 1) * e
+        return jnp.stack([masked(level, p + i, mask) for i in range(c)])
 
     def chunks(where):
         p0, planes, r0, rows = where
@@ -648,37 +650,33 @@
         masks = [
             row_mask(level, first + b, half, 2) if level < DEEPEST else None for b in (0, 1)
         ]
-        mixes = {}
-
-        def mixed(src, index, j, k):
-            key = (index, j, k)
-            if key not in mixes:
-                load = lambda dy: src[x0 + j, k, pl.ds(start + dy, half), :]
-                quarter = 0.25 * load(0)
-                near = load(0) - quarter
-                out = []
-                for dy in (-1, 1):
-                    value = near + 0.25 * load(dy)
-                    far = 0.25 * value
-                    out.append((value - far, far))
-                mixes[key] = out
-            return mixes[key]
-
-        for j in range(low // 2, (high - 1) // 2 + 1):
-            for a in (0, 1):
-                p = 2 * j + a
-                if not low <= p < high:
-                    continue
-                for b in (0, 1):
-                    if level < DEEPEST:
-                        mask = masks[b] * plane_mask(level, p)
-                    for index, (src, dst) in enumerate(coarse):
-                        for k in range(gz_n):
-                            near = mixed(src, index, j, k)[b][0]
-                            value = near + mixed(src, index, j + 2 * a - 1, k)[b][1]
+        def mixed(src, j, k):
+            load = lambda dy: src[x0 + j, k, pl.ds(start + dy, half), :]
+            quarter = 0.25 * load(0)
+            near = load(0) - quarter
+            out = []
+            for dy in (-1, 1):
+                value = near + 0.25 * load(dy)
+                far = 0.25 * value
+                out.append((value - far, far))
+            return out
+
+        first_j, last_j = low // 2, (high - 1) // 2
+        for src, dst in coarse:
+            for k in range(gz_n):
+                behind, here = mixed(src, first_j - 1, k), mixed(src, first_j, k)
+                for j in range(first_j, last_j + 1):
+                    ahead = mixed(src, j + 1, k)
+                    for a, beside in ((0, behind), (1, ahead)):
+                        p = 2 * j + a
+                        if not low <= p < high:
+                            continue
+                        for b in (0, 1):
+                            value = here[b][0] + beside[b][1]
                             if level < DEEPEST:
-                                value = value * mask
+                                value = masked(level, p, value * masks[b])
                             dst[p + shift, k, pl.ds(first + b, half, 2), :] = value
+                    behind, here = here, ahead
 
     def correct(level, coarse_u, coarse_g, x0, y0):
         prolong(level, x0, y0, [(coarse_u, C[level]), (coarse_g, E[level])])
@@ -787,7 +785,7 @@
         arrive = lambda which: settle(h_recv.at[level, which], total(-1, (which,)))
         return start, arrive, lambda: settle(h_send.at[level], total(1, (0, 1)))
 
-    def widen(level, arrive):
+    def gather_halo(level, arrive):
         n0, n1 = owned(level)
         for core in range(gz_n):
             near = near_halos(level, core) or (0, 0, 0)
@@ -808,13 +806,13 @@
                 def _():
                     relay(level)(core).start()
 
+    def presmooth(level):
+        if level:
             relay(level)(0).wait_recv()
         relax(level, X[level][0], X[level][1], region(level, 1))
         relax(level, X[level][1], X[level][2], region(level, 2))
-        if level:
-            relay(level)(0).wait_send()
-
-    def gather_all(meanwhile):
+
+    def gather_all(early, late):
         leader = gz_n - 1
         leading = iz == leader
 
@@ -835,6 +833,11 @@
                 line_y(lax.rem(iy + s, gy_n), iy).start()
             share(own3, iy)
             gather[ix, iy] = own3[...]
+
+        early()
+
+        @pl.when(leading)
+        def _():
             for distance in range(1, gy_n):
                 for y in (iy + distance, iy - distance):
 
@@ -843,7 +846,7 @@
                         line_y(y, y).wait_recv()
                         share(gather.at[ix, y], y)
 
-        meanwhile()
+        late()
         size = own3.shape[0] * own3.shape[1] * own3.shape[2]
 
         @pl.when(leading)
@@ -875,6 +878,8 @@
 
         return drains
 
+    for c in loads:
+        c.start()
     f_load.wait()
     pl.semaphore_wait(barrier, partners)
     send0(0)
@@ -885,11 +890,13 @@
         for c in group[:2]:
             c.start()
     clear_edges()
-    send0(1)
     for group in setups:
         for c in group[:2]:
             c.wait()
     assemble(0, 0)
+    send0(1)
+    for group in setups:
+        group[2].start()
     local_done(0)
 
     def arrive0(which):
@@ -900,7 +907,7 @@
     def later():
         for group in setups:
             group[2].wait()
-        lax.fori_loop(1, levels, assemble, 0)
+        assemble(1, 0)
 
     arrive = arrive0
     drains = [lambda: settle(h_send.at[0], sent0)]
@@ -916,19 +923,37 @@
             start, following, drain = exchange(level + 1)
             drains.append(drain)
             start(0)
-            start(1)
             if level == 0:
-                for group in setups:
-                    group[2].start()
-                widen(level, arrive)
                 later()
+                gather_halo(level, arrive)
+                presmooth(level)
+                start(1)
             else:
+                lax.fori_loop(2, levels, assemble, 0)
                 clear_coarse()
-                widen(level, arrive)
+                start(1)
+
+                @pl.when(iz < gz_n - 1)
+                def _():
+                    gather_halo(level, arrive)
+
+                before = arrive
             arrive = following
         else:
             restrict_planes(level, own3, gz_n * n0, p - extra, r, 0, 0, n1)
-            drains.append(gather_all(lambda: widen(level, arrive)))
+
+            def early():
+                @pl.when(iz == gz_n - 1)
+                def _():
+                    gather_halo(level - 1, before)
+
+                presmooth(level - 1)
+
+            def late():
+                gather_halo(level, arrive)
+                presmooth(level)
+
+            drains.append(gather_all(early, late))
 
     whole3, whole4 = region(3, 0), region(4, 0)
     spread(3, X[3][0], whole3)
@@ -978,6 +1003,8 @@
     send_out(res_ref, 0, nx)
     for drain in drains:
         drain()
+    for level in range(1, DEEPEST):
+        relay(level)(0).wait_send()
     for sem in (o_send, o_recv):
         take_rows(sem, (gz_n - 1) * 2 * nx * ny)
 
@@ -1083,7 +1110,7 @@
             collective_id=0, has_side_effects=True, vmem_limit_bytes=48 * 1024 * 1024
         ),
     )(hold(right_side), hold(z_faces.reshape(1, -1)), hold(xy_coupling), hold(block_inverse))
-    pieces = 4
+    pieces = 2
     return tuple(
         pl.pallas_call(
             functools.partial(store_kernel, pieces),

time: 31.7 us -> 29.8 us (0.940)
  Pallas kernels: 31 us -> 29 us
    pallas_call x1, Pallas kernels: 29.9 us -> 28 us  [fused_body(): pl.pallas_call(functools.partial(cycle_kernel, (gx_n, gy_n, gz_n, nx, ny,...]
where the time goes in v5:
time: 29.8 us; the launch traced here: 29.6 us
  Pallas kernels  29 us (97%)
  between operations  0.64 us (2%)
    pallas_call x1, Pallas kernels, fused_body(): pl.pallas_call(functools.partial(cycle_kernel, (gx_n, gy_n, gz_n, nx, ny,...  28 us
    pallas_call x1, Pallas kernels, fused_body(): pl.pallas_call(functools.partial(store_kernel, pieces), out_shape=[jax.Sh...  1 us

profile of v5, /device:TPU:0, one launch (start us, length us, event | category | flops | bytes accessed | tf_op | source)
XLA Modules:
  0.0 29.6 jit_solution(14845842129330984822)
XLA Ops:
  0.6 28.0 %shard_map.59 = (f32[2,32,32,128]{3,2,1,0:T(8,128)S(1)}, f32[2,32,32,128]{3,2,1,0:T(8,128)S(1)}) custom-call(f32[32,32,128]{2,1,0:T(8,128)} %f_hbm.1, f32[1,128]{1,0:T(1,128)} %bitcast.1, f32[5]{0:T(128)} %e_hbm.1, f32[5,128,128]{2,1,0:T(8,128)} %g_hbm.1), custom_call_target="tpu_custom_call" | custom-call | tf_op jit(solution)/shard_map/pallas_call | solution.py:1098
  28.6 1.0 %shard_map.60 = (f32[32,32,128]{2,1,0:T(8,128)}, f32[32,32,128]{2,1,0:T(8,128)}) custom-call(f32[2,32,32,128]{3,2,1,0:T(8,128)S(1)} %get-tuple-element.4.sol_v, f32[2,32,32,128]{3,2,1,0:T(8,128)S(1)} %get-tuple-element.5.res_v), custom_call_target="tpu_custom_call" | custom-call | tf_op jit(solution)/shard_map/pallas_call | solution.py:1115

commit v6 on v5

--- a/solution.py
+++ b/solution.py
@@ -231,7 +231,7 @@
 
 
 def split_planes(count, rows):
-    return max(c for c in range(1, count + 1) if count % c == 0 and c * rows <= 448)
+    return max(c for c in range(1, count + 1) if count % c == 0 and c * rows <= 520)
 
 
 def cycle_kernel(geometry, f_hbm, z_hbm, e_hbm, g_hbm, sol_ref, res_ref, *scratch):
@@ -294,30 +294,33 @@
     )
     barrier = pltpu.get_barrier_semaphore()
     partners = jnp.int32(0)
-    for dx in range(1 - bx_n, bx_n):
-        for dy in range(1 - gy_n, gy_n):
-            close = abs(dx) <= reach_all and abs(dy) <= 1
-            if (dx == 0 and dy == 0) or not close:
-                continue
-            x, y = bx + dx, iy + dy
-            ok = (x >= 0) & (x < bx_n) & (y >= 0) & (y < gy_n)
-
-            @pl.when(ok)
-            def _():
-                pl.semaphore_signal(
-                    barrier,
-                    inc=1,
-                    device_id=(x // gz_n, y, lax.rem(x, gz_n)),
-                    device_id_type=MESH,
-                )
-
-            partners = partners + jnp.where(ok, 1, 0).astype(jnp.int32)
+    offsets = [
+        (dx, dy)
+        for dx in range(-reach_all, reach_all + 1)
+        for dy in (-1, 0, 1)
+        if dx or dy
+    ]
+    offsets.sort(key=lambda offset: -abs(offset[0]) - 2 * abs(offset[1]))
+    for dx, dy in offsets:
+        x, y = bx + dx, iy + dy
+        ok = (x >= 0) & (x < bx_n) & (y >= 0) & (y < gy_n)
+
+        @pl.when(ok)
+        def _():
+            pl.semaphore_signal(
+                barrier,
+                inc=1,
+                device_id=(x // gz_n, y, lax.rem(x, gz_n)),
+                device_id_type=MESH,
+            )
+
+        partners = partners + jnp.where(ok, 1, 0).astype(jnp.int32)
 
     def setup_copies(other):
         here = (ix, iy, lax.rem(iz + other, gz_n))
         out = []
         for i, block in enumerate((z_all.at[iz], g_all.at[0, iz], g_all.at[rest, iz])):
-            out.append(copy(block, block, g_send.at[other, i], g_recv.at[other, i], here))
+            out.append(copy(block, block, g_send.at[i], g_recv.at[i], here))
         return out
 
     def runs(count, key):
@@ -812,7 +815,7 @@
         relax(level, X[level][0], X[level][1], region(level, 1))
         relax(level, X[level][1], X[level][2], region(level, 2))
 
-    def gather_all(early, late):
+    def gather_all(late):
         leader = gz_n - 1
         leading = iz == leader
 
@@ -833,11 +836,6 @@
                 line_y(lax.rem(iy + s, gy_n), iy).start()
             share(own3, iy)
             gather[ix, iy] = own3[...]
-
-        early()
-
-        @pl.when(leading)
-        def _():
             for distance in range(1, gy_n):
                 for y in (iy + distance, iy - distance):
 
@@ -927,9 +925,10 @@
                 later()
                 gather_halo(level, arrive)
                 presmooth(level)
-                start(1)
+                behind = start
             else:
                 lax.fori_loop(2, levels, assemble, 0)
+                behind(1)
                 clear_coarse()
                 start(1)
 
@@ -942,18 +941,16 @@
         else:
             restrict_planes(level, own3, gz_n * n0, p - extra, r, 0, 0, n1)
 
-            def early():
+            def late():
                 @pl.when(iz == gz_n - 1)
                 def _():
                     gather_halo(level - 1, before)
 
                 presmooth(level - 1)
-
-            def late():
                 gather_halo(level, arrive)
                 presmooth(level)
 
-            drains.append(gather_all(early, late))
+            drains.append(gather_all(late))
 
     whole3, whole4 = region(3, 0), region(4, 0)
     spread(3, X[3][0], whole3)
@@ -1086,7 +1083,7 @@
         + [vmem(w) for w in windows[: DEEPEST + 1]]
         + [vmem(w) for w in windows[:DEEPEST]]
         + [dma((7,))]
-        + [dma((gz_n, 3))] * 2
+        + [dma((3,))] * 2
         + [dma((DEEPEST,)), dma((DEEPEST, 2))]
         + [dma((gy_n,)), dma((5,))]
         + [dma((DEEPEST - 1,))] * 2

time: 29.8 us -> 29.6 us (level)
  no operation moved by 1% of the time
where the time goes in v6:
time: 29.6 us; the launch traced here: 29.4 us
  Pallas kernels  28.8 us (97%)
  between operations  0.64 us (2%)
    pallas_call x1, Pallas kernels, fused_body(): pl.pallas_call(functools.partial(cycle_kernel, (gx_n, gy_n, gz_n, nx, ny,...  27.8 us
    pallas_call x1, Pallas kernels, fused_body(): pl.pallas_call(functools.partial(store_kernel, pieces), out_shape=[jax.Sh...  1 us

profile of v6, /device:TPU:0, one launch (start us, length us, event | category | flops | bytes accessed | tf_op | source)
XLA Modules:
  0.0 29.4 jit_solution(8249202397459806434)
XLA Ops:
  0.6 27.8 %shard_map.59 = (f32[2,32,32,128]{3,2,1,0:T(8,128)S(1)}, f32[2,32,32,128]{3,2,1,0:T(8,128)S(1)}) custom-call(f32[32,32,128]{2,1,0:T(8,128)} %f_hbm.1, f32[1,128]{1,0:T(1,128)} %bitcast.1, f32[5]{0:T(128)} %e_hbm.1, f32[5,128,128]{2,1,0:T(8,128)} %g_hbm.1), custom_call_target="tpu_custom_call" | custom-call | tf_op jit(solution)/shard_map/pallas_call | solution.py:1095
  28.4 1.0 %shard_map.60 = (f32[32,32,128]{2,1,0:T(8,128)}, f32[32,32,128]{2,1,0:T(8,128)}) custom-call(f32[2,32,32,128]{3,2,1,0:T(8,128)S(1)} %get-tuple-element.4.sol_v, f32[2,32,32,128]{3,2,1,0:T(8,128)S(1)} %get-tuple-element.5.res_v), custom_call_target="tpu_custom_call" | custom-call | tf_op jit(solution)/shard_map/pallas_call | solution.py:1112

commit v7 on v6

--- a/solution.py
+++ b/solution.py
@@ -832,8 +832,13 @@
 
         @pl.when(leading)
         def _():
-            for s in range(1, gy_n):
-                line_y(lax.rem(iy + s, gy_n), iy).start()
+            for distance in range(gy_n - 1, 0, -1):
+                for y in (iy + distance, iy - distance):
+
+                    @pl.when((y >= 0) & (y < gy_n))
+                    def _():
+                        line_y(y, iy).start()
+
             share(own3, iy)
             gather[ix, iy] = own3[...]
             for distance in range(1, gy_n):

time: 29.6 us -> 29.6 us (level)
  no operation moved by 1% of the time
where the time goes in v7:
time: 29.6 us; the launch traced here: 29.4 us
  Pallas kernels  28.8 us (97%)
  between operations  0.64 us (2%)
    pallas_call x1, Pallas kernels, fused_body(): pl.pallas_call(functools.partial(cycle_kernel, (gx_n, gy_n, gz_n, nx, ny,...  27.8 us
    pallas_call x1, Pallas kernels, fused_body(): pl.pallas_call(functools.partial(store_kernel, pieces), out_shape=[jax.Sh...  1 us

profile of v7, /device:TPU:0, one launch (start us, length us, event | category | flops | bytes accessed | tf_op | source)
XLA Modules:
  0.0 29.4 jit_solution(7351082072684783139)
XLA Ops:
  0.6 27.8 %shard_map.59 = (f32[2,32,32,128]{3,2,1,0:T(8,128)S(1)}, f32[2,32,32,128]{3,2,1,0:T(8,128)S(1)}) custom-call(f32[32,32,128]{2,1,0:T(8,128)} %f_hbm.1, f32[1,128]{1,0:T(1,128)} %bitcast.1, f32[5]{0:T(128)} %e_hbm.1, f32[5,128,128]{2,1,0:T(8,128)} %g_hbm.1), custom_call_target="tpu_custom_call" | custom-call | tf_op jit(solution)/shard_map/pallas_call | solution.py:1100
  28.4 1.0 %shard_map.60 = (f32[32,32,128]{2,1,0:T(8,128)}, f32[32,32,128]{2,1,0:T(8,128)}) custom-call(f32[2,32,32,128]{3,2,1,0:T(8,128)S(1)} %get-tuple-element.4.sol_v, f32[2,32,32,128]{3,2,1,0:T(8,128)S(1)} %get-tuple-element.5.res_v), custom_call_target="tpu_custom_call" | custom-call | tf_op jit(solution)/shard_map/pallas_call | solution.py:1117
